TPU v7x, 32 devices: a whole 2x2x4 slice. The times are simulated.
32 devices in a mesh: pass: 4 (over y, x), red: 4 (over z), grp: 2 (over core).
Axes of the slice: x: 2, y: 2, z: 4, core: 2. Of those that a mesh axis runs over, the one named last changes fastest.
Arguments:
- query_lex: bfloat16 [1536, 16384], P(None, 'red')
- query_dense: bfloat16 [1536, 4096], P(None, 'red')
- passage_lex: bfloat16 [4096, 16384], P(('pass', 'grp'), 'red'), may hold values from 0 to 0.47
- passage_dense: bfloat16 [4096, 4096], P(('pass', 'grp'), 'red'), may hold values from -1.33 to 1.33
- positives: int32 [1536], replicated, may hold values from 0 to 4095
Outputs:
- loss_rows: float32 [1536], P('red')
- grad_query_lex: float32 [1536, 16384], P(('pass', 'grp'), 'red')
- grad_query_dense: float32 [1536, 4096], P(('pass', 'grp'), 'red')
- grad_passage_lex: float32 [4096, 16384], P(('pass', 'grp'), 'red')
- grad_passage_dense: float32 [4096, 4096], P(('pass', 'grp'), 'red')
All inputs are finite; a program needn't handle non-finite values.
Results may differ from a plain program's by a relative error of at most 0.0022.
Values may be sent and summed in bfloat16 or wider, within the bound.
A program may use at most 192 MiB of HBM per device.

v0:
```python
import jax
import jax.numpy as jnp
from jax import lax
from jax.sharding import PartitionSpec as P


def contract_rows(first, second):
    return lax.dot_general(
        first, second, (((1,), (1,)), ((), ())), preferred_element_type=jnp.float32
    )


def contract_columns(first, second):
    return lax.dot_general(
        first, second, (((0,), (0,)), ((), ())), preferred_element_type=jnp.float32
    )


def turn(count, step):
    return [(i, (i + step) % count) for i in range(count)]


def from_chip(rows):
    count = lax.axis_size("grp")
    pieces = [rows]
    for step in range(1, count):
        pieces.append(lax.ppermute(rows, "grp", turn(count, step)))
    return jnp.concatenate(pieces, axis=0)


def on_device(query_lex, query_dense, passage_lex, passage_dense, positives):
    chip_passage_lex = from_chip(passage_lex)
    chip_passage_dense = from_chip(passage_dense)
    lex_partial = contract_rows(query_lex, passage_lex)
    dense_partial = contract_rows(query_dense, passage_dense)
    red_count = lax.axis_size("red")
    red_place = lax.axis_index("red")
    own_queries = query_lex.shape[0] // red_count
    local_passages = passage_lex.shape[0]
    first_column = lax.axis_index(("pass", "grp")) * local_passages
    lexical, dense_logit = (
        lax.psum_scatter(lex_partial, "red", scatter_dimension=0, tiled=True),
        lax.psum_scatter(dense_partial, "red", scatter_dimension=0, tiled=True),
    )
    first_query = red_place * own_queries
    query_count = lexical.shape[0]
    targets = lax.dynamic_slice_in_dim(positives, first_query, query_count)
    columns = first_column + lax.broadcasted_iota(jnp.int32, (1, local_passages), 1)
    target_mask = (targets[:, None] == columns).astype(jnp.float32)
    joined_logit = dense_logit + 0.3 * lexical
    scores = (joined_logit, dense_logit, lexical)
    local_max = tuple((jnp.max(logits, axis=1) for logits in scores))
    powers = tuple((jnp.exp(scores[slot] - local_max[slot][:, None]) for slot in range(3)))
    stats = jnp.stack(
        local_max
        + tuple((jnp.sum(power, axis=1) for power in powers))
        + (
            jnp.sum(powers[0] * (joined_logit - dense_logit), axis=1),
            jnp.sum(powers[0] * (joined_logit - lexical), axis=1),
        )
        + tuple((jnp.sum(target_mask * logits, axis=1) for logits in scores))
    )
    everyone = lax.all_gather(stats, ("pass", "grp"), axis=0)
    maxima = jnp.max(everyone[:, 0:3], axis=0)
    factors = jnp.exp(everyone[:, 0:3] - maxima)
    totals = jnp.sum(factors * everyone[:, 3:6], axis=0)
    weighted = jnp.sum(factors[:, 0:1] * everyone[:, 6:8], axis=0)
    picked_all = jnp.sum(everyone[:, 8:11], axis=0)
    log_totals = tuple((maxima[slot] + jnp.log(totals[slot]) for slot in range(3)))
    probability = tuple((jnp.exp(scores[slot] - log_totals[slot][:, None]) for slot in range(3)))
    kl_dense = weighted[0] / totals[0] - log_totals[0] + log_totals[1]
    kl_lex = weighted[1] / totals[0] - log_totals[0] + log_totals[2]
    loss_rows = (
        log_totals[0]
        - picked_all[0]
        + 0.5 * (log_totals[1] - picked_all[1])
        + 0.5 * (log_totals[2] - picked_all[2])
        + 0.5 * kl_dense
        + 0.5 * kl_lex
    )
    grad_dense = (0.5 * probability[0] + probability[1] - 1.5 * target_mask).astype(jnp.bfloat16)
    grad_lex = (-0.2 * probability[0] + probability[2] - 0.8 * target_mask).astype(jnp.bfloat16)
    grad_dense, grad_lex = (
        lax.all_gather(grad_dense, "red", axis=0, tiled=True),
        lax.all_gather(grad_lex, "red", axis=0, tiled=True),
    )
    pass_count = lax.axis_size("pass")
    pass_place = lax.axis_index("pass")
    grp_count = lax.axis_size("grp")
    grp_place = lax.axis_index("grp")
    block = query_lex.shape[0] // (pass_count * grp_count)

    def for_core(grads, core):
        blocks = grads.reshape(pass_count, grp_count, block, grads.shape[1])
        return lax.dynamic_index_in_dim(blocks, core, 1, keepdims=False)

    def with_chip(grads):
        pieces = [for_core(grads, grp_place)]
        for step in range(1, grp_count):
            away = for_core(grads, lax.rem(grp_place + step, grp_count))
            pieces.append(lax.ppermute(away, "grp", turn(grp_count, step)))
        return jnp.concatenate(pieces, axis=2)

    chip_lex = with_chip(grad_lex)
    chip_dense = with_chip(grad_dense)

    def query_terms(place):
        return (
            jnp.dot(
                lax.dynamic_index_in_dim(chip_lex, place, 0, keepdims=False),
                chip_passage_lex,
                preferred_element_type=jnp.float32,
            ),
            jnp.dot(
                lax.dynamic_index_in_dim(chip_dense, place, 0, keepdims=False),
                chip_passage_dense,
                preferred_element_type=jnp.float32,
            ),
        )

    power_of_two = pass_count & (pass_count - 1) == 0
    leaving = []
    for step in reversed(range(1, pass_count)):
        place = (
            lax.bitwise_xor(pass_place, step)
            if power_of_two
            else lax.rem(pass_place + step, pass_count)
        )
        perm = (
            [(i, i ^ step) for i in range(pass_count)]
            if power_of_two
            else [(i, (i + step) % pass_count) for i in range(pass_count)]
        )
        terms = tuple(term.astype(jnp.bfloat16) for term in query_terms(place))
        leaving.append((terms, perm))
    sent = tuple(terms for terms, _ in leaving)
    sent, grad_lex, grad_dense, chip_lex, chip_dense = lax.optimization_barrier(
        (sent, grad_lex, grad_dense, chip_lex, chip_dense)
    )
    arrived = [
        tuple(lax.ppermute(term, "pass", perm) for term in terms)
        for terms, (_, perm) in zip(sent, leaving)
    ]
    grad_passage_lex = contract_columns(grad_lex, query_lex)
    grad_passage_dense = contract_columns(grad_dense, query_dense)
    grad_query_lex, grad_query_dense = query_terms(pass_place)
    for term_lex, term_dense in arrived:
        grad_query_lex = grad_query_lex + term_lex.astype(jnp.float32)
        grad_query_dense = grad_query_dense + term_dense.astype(jnp.float32)
    return (
        loss_rows,
        grad_query_lex,
        grad_query_dense,
        grad_passage_lex,
        grad_passage_dense,
    )


def solution(mesh):
    return jax.shard_map(
        on_device,
        mesh=mesh,
        in_specs=(
            P(None, "red"),
            P(None, "red"),
            P(("pass", "grp"), "red"),
            P(("pass", "grp"), "red"),
            P(),
        ),
        out_specs=(
            P("red"),
            P(("pass", "grp"), "red"),
            P(("pass", "grp"), "red"),
            P(("pass", "grp"), "red"),
            P(("pass", "grp"), "red"),
        ),
        check_vma=False,
    )
```

profile of v0, /device:TPU:1, one launch (start us, length us, event | category | flops | bytes accessed | tf_op | source)
XLA Modules:
  0.0 359.5 jit_solution(1406312510967911010)
XLA Ops:
  7.2 0.0 copy-start
  7.2 0.0 reduce-scatter.5.cloned.1.call-start
  7.2 12.2 %fusion.60 = f32[1536,512]{1,0:T(8,128)} fusion(bf16[1536,4096]{1,0:T(8,128)(2,1)} %param.5, bf16[512,4096]{1,0:T(8,128)(2,1)} %param.7), kind=kOutput, calls=%fused_computation.112 | convolution fusion | flops 6442450944 | bytes 19922944 | tf_op jit(solution)/shard_map/dot_general | solution.py:8
  19.4 0.0 reduce-scatter.5.cloned.1.call-update
  19.4 0.0 reduce-scatter.3.cloned.1.call-start
  19.5 4.7 %fusion.59 = f32[1536,512]{1,0:T(8,128)} fusion(bf16[1536,1024]{1,0:T(8,128)(2,1)S(1)} %copy-done, bf16[512,1024]{1,0:T(8,128)(2,1)} %param.8), kind=kOutput, calls=%fused_computation.111 | convolution fusion | flops 1610612736 | bytes 7340032 | tf_op jit(solution)/shard_map/dot_general | solution.py:8
  24.2 0.0 reduce-scatter.3.cloned.1.call-update
  24.3 0.0 all-gather.5.cloned.1.call-start
  24.3 0.1 collective-permute-start.1
  24.4 0.8 dynamic_slice.41
  25.2 56.5 %reduce-scatter.5.cloned.1.call-done = f32[384,512]{1,0:T(8,128)} async-done(((f32[1536,512]{1,0:T(8,128)}), f32[384,512]{1,0:T(8,128)}) %reduce-scatter.5.cloned.1.call-update) | async-done | bytes 786448 | tf_op jit(solution)/shard_map/reduce_scatter | solution.py:42
  81.7 63.2 %reduce-scatter.3.cloned.1.call-done = f32[384,512]{1,0:T(8,128)} async-done(((f32[1536,512]{1,0:T(8,128)}), f32[384,512]{1,0:T(8,128)}) %reduce-scatter.3.cloned.1.call-update) | async-done | bytes 786448 | tf_op jit(solution)/shard_map/reduce_scatter | solution.py:43
  144.9 1.7 fusion.58
  146.6 2.5 multiply_reduce_fusion
  149.1 0.1 stack.47
  149.2 10.1 %all-gather.1 = f32[8,11,384]{2,1,0:T(8,128)S(1)} all-gather(f32[1,11,384]{2,1,0:T(8,128)S(1)} %bitcast.58), channel_id=2, replica_groups=mesh['pass'=4,'red'=4,'grp'=2] {'pass','grp'}, dimensions={0}, use_global_device_ids=true | all-gather | bytes 152064 | tf_op jit(solution)/shard_map/all_gather | solution.py:63
  159.4 0.1 slice_reduce_fusion.4
  159.5 2.9 fusion.10
  162.4 0.0 all-gather.5.cloned.1.call-update
  162.4 0.2 all-gather.7.cloned.1.call-start
  162.6 0.3 all-gather.7.cloned.1.call-update
  163.0 0.2 collective-permute-start.3
  163.2 2.3 constant_dynamic-update-slice_fusion.3
  165.5 4.7 %constant_dynamic-update-slice_fusion.1 = bf16[1024,4096]{1,0:T(8,128)(2,1)} fusion(bf16[512,4096]{1,0:T(8,128)(2,1)} %param.7), kind=kLoop, calls=%fused_computation.75 | loop fusion | bytes 8388608
  170.1 0.0 collective-permute-done.3
  170.2 2.3 constant_dynamic-update-slice_fusion.2
  172.4 24.8 %all-gather.5.cloned.1.call-done = bf16[1536,512]{1,0:T(8,128)(2,1)} async-done(((bf16[384,512]{1,0:T(8,128)(2,1)}), bf16[1536,512]{1,0:T(8,128)(2,1)}) %all-gather.5.cloned.1.call-update) | async-done | bytes 1572880 | tf_op jit(solution)/shard_map/all_gather | solution.py:85
  197.2 2.6 dynamic-slice_bitcast_fusion.2
  199.8 1.6 collective-permute-start
  201.3 0.0 collective-permute-done.1
  201.3 4.7 %constant_dynamic-update-slice_fusion = bf16[1024,4096]{1,0:T(8,128)(2,1)} fusion(bf16[1024,4096]{1,0:T(8,128)(2,1)} %constant_dynamic-update-slice_fusion.1, bf16[512,4096]{1,0:T(8,128)(2,1)} %collective-permute-done.1), kind=kLoop, calls=%fused_computation.74 | loop fusion | bytes 8388608 | tf_op jit(solution)/shard_map/concatenate | solution.py:28
  206.0 0.6 multiply_add_fusion.1
  206.6 27.9 %all-gather.7.cloned.1.call-done = bf16[1536,512]{1,0:T(8,128)(2,1)} async-done(((bf16[384,512]{1,0:T(8,128)(2,1)}), bf16[1536,512]{1,0:T(8,128)(2,1)}) %all-gather.7.cloned.1.call-update) | async-done | bytes 1572880 | tf_op jit(solution)/shard_map/all_gather | solution.py:84
  234.5 1.7 dynamic-slice_bitcast_fusion
  236.2 1.6 collective-permute-start.2
  237.8 0.0 collective-permute-done
  237.8 5.4 %convolution_convert_fusion.2 = bf16[192,4096]{1,0:T(8,128)(2,1)S(1)} fusion(bf16[1024,4096]{1,0:T(8,128)(2,1)} %constant_dynamic-update-slice_fusion, s32[]{:T(128)S(6)} %select_n.32, bf16[4,192,512]{2,1,0:T(8,128)(2,1)S(1)} %copy-done.1, bf16[4,192,512]{2,1,0:T(8,128)(2,1)} %collective-permute-done), kind=kOutput, calls=%fused_computation.5 | convolution fusion | flops 1612185600 | bytes 11534340 | tf_op jit(solution)/shard_map/dot_general | solution.py:109
  243.3 0.0 slice-done
  243.3 0.0 slice-done.1
  243.3 2.8 convolution_convert_fusion.1
  246.1 0.0 collective-permute-done.2
  246.1 2.2 convolution_convert_fusion.5
  248.3 2.2 convolution_convert_fusion.4
  250.4 2.7 convolution_convert_fusion
  253.2 2.2 convolution_convert_fusion.3
  255.4 1.3 pad_maximum_fusion
  256.7 0.2 pad_maximum_fusion.1
  256.9 1.2 collective-permute-start.6
  258.2 1.2 collective-permute-start.5
  259.4 0.3 collective-permute-start.4
  259.7 1.2 collective-permute-start.9
  260.8 1.2 collective-permute-start.8
  262.0 0.0 copy-done.2
  262.0 11.8 %fusion.61 = f32[512,4096]{1,0:T(8,128)} fusion(bf16[1536,512]{1,0:T(8,128)(2,1)S(1)} %copy-done.2, bf16[1536,4096]{1,0:T(8,128)(2,1)} %param.5), kind=kOutput, calls=%fused_computation.113 | convolution fusion | flops 6442450944 | bytes 22544384 | tf_op jit(solution)/shard_map/dot_general | solution.py:14
  273.8 61.3 %collective-permute-done.9 = bf16[192,1024]{1,0:T(8,128)(2,1)S(1)} collective-permute-done((bf16[192,1024]{1,0:T(8,128)(2,1)S(1)}, bf16[192,1024]{1,0:T(8,128)(2,1)S(1)}, u32[]{:S(2)}, u32[]{:S(2)}) %collective-permute-start.9) | collective-permute-done | bytes 393248 | tf_op jit(solution)/shard_map/ppermute | solution.py:141
  335.1 2.1 collective-permute-start.7
  337.2 3.1 fusion.62
  340.3 0.0 collective-permute-done.8
  340.3 5.4 %collective-permute-done.7 = bf16[192,1024]{1,0:T(8,128)(2,1)S(1)} collective-permute-done((bf16[192,1024]{1,0:T(8,128)(2,1)S(1)}, bf16[192,1024]{1,0:T(8,128)(2,1)S(1)}, u32[]{:S(2)}, u32[]{:S(2)}) %collective-permute-start.7) | collective-permute-done | bytes 393248 | tf_op jit(solution)/shard_map/ppermute | solution.py:141
  345.7 3.2 fusion.3
  348.9 0.0 collective-permute-done.6
  348.9 0.0 collective-permute-done.5
  348.9 0.0 collective-permute-done.4
  348.9 4.1 %fusion.1 = f32[192,4096]{1,0:T(8,128)} fusion(bf16[1024,4096]{1,0:T(8,128)(2,1)S(1)} %bitcast.55, bf16[192,4096]{1,0:T(8,128)(2,1)S(1)} %collective-permute-done.6, bf16[192,4096]{1,0:T(8,128)(2,1)S(1)} %collective-permute-done.5, bf16[192,4096]{1,0:T(8,128)(2,1)S(1)} %collective-permute-done.4, bf16[4,192,1024]{2,1,0:T(8,128)(2,1)S(1)} %pad_maximum_fusion, ...), kind=kOutput, calls=%fused_computation.2 | convolution fusion | flops 1615331328 | bytes 16646148 | tf_op jit(solution)/shard_map/dot_general | solution.py:109
  (26 shorter events, 0.2 us)
Async XLA Ops:
  7.2 12.3 %copy-start = (bf16[1536,1024]{1,0:T(8,128)(2,1)S(1)}, bf16[1536,1024]{1,0:T(8,128)(2,1)}, u32[]{:S(2)}) copy-start(bf16[1536,1024]{1,0:T(8,128)(2,1)} %param.6) | copy-start | bytes 9437188
  7.2 74.5 %reduce-scatter.5.cloned.1.call-start = ((), (), s32[]{:S(2)}) async-start(), calls=%async_computation.3 | async-start | bytes 3932160 | tf_op jit(solution)/shard_map/reduce_scatter | solution.py:42
  19.4 125.5 %reduce-scatter.3.cloned.1.call-start = ((), (), s32[]{:S(2)}) async-start(), calls=%async_computation.2 | async-start | bytes 3932160 | tf_op jit(solution)/shard_map/reduce_scatter | solution.py:43
  24.3 172.9 %all-gather.5.cloned.1.call-start = ((), (), s32[]{:S(2)}) async-start(), calls=%async_computation.4 | async-start | bytes 1966080 | tf_op jit(solution)/shard_map/all_gather | solution.py:85
  24.3 177.0 %collective-permute-start.1 = (bf16[512,4096]{1,0:T(8,128)(2,1)}, bf16[512,4096]{1,0:T(8,128)(2,1)}, u32[]{:S(2)}, u32[]{:S(2)}) collective-permute-start(bf16[512,4096]{1,0:T(8,128)(2,1)} %param.7), channel_id=1, source_target_pairs={{0,1},{1,0},{2,3},{3,2},{4,5},{5,4},{6,7},{7,6},{8,9},{9,8},{10,11... | collective-permute-start | bytes 12582920 | tf_op jit(solution)/shard_map/ppermute | solution.py:27
  162.4 72.1 %all-gather.7.cloned.1.call-start = ((), (), s32[]{:S(2)}) async-start(), calls=%async_computation.5 | async-start | bytes 1966080 | tf_op jit(solution)/shard_map/all_gather | solution.py:84
  163.0 7.2 %collective-permute-start.3 = (bf16[512,1024]{1,0:T(8,128)(2,1)}, bf16[512,1024]{1,0:T(8,128)(2,1)}, u32[]{:S(2)}, u32[]{:S(2)}) collective-permute-start(bf16[512,1024]{1,0:T(8,128)(2,1)} %param.8), channel_id=1, source_target_pairs={{0,1},{1,0},{2,3},{3,2},{4,5},{5,4},{6,7},{7,6},{8,9},{9,8},{10,11... | collective-permute-start | bytes 3145736 | tf_op jit(solution)/shard_map/ppermute | solution.py:27
  199.8 38.1 %collective-permute-start = (bf16[4,192,512]{2,1,0:T(8,128)(2,1)}, bf16[4,192,512]{2,1,0:T(8,128)(2,1)}, u32[]{:S(2)}, u32[]{:S(2)}) collective-permute-start(bf16[4,192,512]{2,1,0:T(8,128)(2,1)} %get-tuple-element.54), channel_id=1, source_target_pairs={{0,1},{1,0},{2,3},{3,2},{4,5},{5,4},{6,7},{7,6},{8,9},{9,8},{10,11... | collective-permute-start | bytes 2359304 | tf_op jit(solution)/shard_map/ppermute | solution.py:101
  234.5 3.3 copy-start.1
  234.5 8.8 %slice-start = ((s8[8388608]{0:T(1024)(128)(4,1)}), s8[4194304]{0:T(1024)(128)(4,1)S(1)}, s32[]{:S(2)}) async-start(s8[8388608]{0:T(1024)(128)(4,1)} %bitcast.54), calls=%async_computation.6 | async-start | bytes 8388608
  236.2 9.9 %collective-permute-start.2 = (bf16[4,192,512]{2,1,0:T(8,128)(2,1)S(1)}, bf16[4,192,512]{2,1,0:T(8,128)(2,1)S(1)}, u32[]{:S(2)}, u32[]{:S(2)}) collective-permute-start(bf16[4,192,512]{2,1,0:T(8,128)(2,1)S(1)} %get-tuple-element.52), channel_id=1, source_target_pairs={{0,1},{1,0},{2,3},{3,2},{4,5},{5,4},{6,7},{7,6},{8,9},{9,8},{10,11... | collective-permute-start | bytes 2359304 | tf_op jit(solution)/shard_map/ppermute | solution.py:101
  237.8 5.5 %slice-start.1 = ((s8[8388608]{0:T(1024)(128)(4,1)}), s8[4194304]{0:T(1024)(128)(4,1)S(1)}, s32[]{:S(2)}) async-start(s8[8388608]{0:T(1024)(128)(4,1)} %bitcast.54), calls=%async_computation.7 | async-start | bytes 8388608
  256.7 5.3 %copy-start.2 = (bf16[1536,512]{1,0:T(8,128)(2,1)S(1)}, bf16[1536,512]{1,0:T(8,128)(2,1)}, u32[]{:S(2)}) copy-start(bf16[1536,512]{1,0:T(8,128)(2,1)} %all-gather.5.cloned.1.call-done) | copy-start | bytes 4718596
  256.9 80.3 %copy-start.3 = (bf16[1536,512]{1,0:T(8,128)(2,1)S(1)}, bf16[1536,512]{1,0:T(8,128)(2,1)}, u32[]{:S(2)}) copy-start(bf16[1536,512]{1,0:T(8,128)(2,1)} %all-gather.7.cloned.1.call-done) | copy-start | bytes 4718596
  256.9 92.0 %collective-permute-start.6 = (bf16[192,4096]{1,0:T(8,128)(2,1)S(1)}, bf16[192,4096]{1,0:T(8,128)(2,1)S(1)}, u32[]{:S(2)}, u32[]{:S(2)}) collective-permute-start(bf16[192,4096]{1,0:T(8,128)(2,1)S(1)} %convolution_convert_fusion), channel_id=1, source_target_pairs={{0,8},{8,0},{16,24},{24,16},{1,9},{9,1},{17,25},{25,17},{2,10},{10... | collective-permute-start | bytes 4718600 | tf_op jit(solution)/shard_map/ppermute | solution.py:141
  258.2 90.7 %collective-permute-start.5 = (bf16[192,4096]{1,0:T(8,128)(2,1)S(1)}, bf16[192,4096]{1,0:T(8,128)(2,1)S(1)}, u32[]{:S(2)}, u32[]{:S(2)}) collective-permute-start(bf16[192,4096]{1,0:T(8,128)(2,1)S(1)} %convolution_convert_fusion.1), channel_id=1, source_target_pairs={{0,16},{8,24},{16,0},{24,8},{1,17},{9,25},{17,1},{25,9},{2,18},{10... | collective-permute-start | bytes 4718600 | tf_op jit(solution)/shard_map/ppermute | solution.py:141
  259.4 89.5 %collective-permute-start.4 = (bf16[192,4096]{1,0:T(8,128)(2,1)S(1)}, bf16[192,4096]{1,0:T(8,128)(2,1)S(1)}, u32[]{:S(2)}, u32[]{:S(2)}) collective-permute-start(bf16[192,4096]{1,0:T(8,128)(2,1)S(1)} %convolution_convert_fusion.2), channel_id=1, source_target_pairs={{0,24},{8,16},{16,8},{24,0},{1,25},{9,17},{17,9},{25,1},{2,26},{10... | collective-permute-start | bytes 4718600 | tf_op jit(solution)/shard_map/ppermute | solution.py:141
  259.7 75.4 %collective-permute-start.9 = (bf16[192,1024]{1,0:T(8,128)(2,1)S(1)}, bf16[192,1024]{1,0:T(8,128)(2,1)S(1)}, u32[]{:S(2)}, u32[]{:S(2)}) collective-permute-start(bf16[192,1024]{1,0:T(8,128)(2,1)S(1)} %convolution_convert_fusion.3), channel_id=1, source_target_pairs={{0,8},{8,0},{16,24},{24,16},{1,9},{9,1},{17,25},{25,17},{2,10},{10... | collective-permute-start | bytes 1179656 | tf_op jit(solution)/shard_map/ppermute | solution.py:141
  260.8 79.5 %collective-permute-start.8 = (bf16[192,1024]{1,0:T(8,128)(2,1)S(1)}, bf16[192,1024]{1,0:T(8,128)(2,1)S(1)}, u32[]{:S(2)}, u32[]{:S(2)}) collective-permute-start(bf16[192,1024]{1,0:T(8,128)(2,1)S(1)} %convolution_convert_fusion.4), channel_id=1, source_target_pairs={{0,16},{8,24},{16,0},{24,8},{1,17},{9,25},{17,1},{25,9},{2,18},{10... | collective-permute-start | bytes 1179656 | tf_op jit(solution)/shard_map/ppermute | solution.py:141
  335.1 10.7 %collective-permute-start.7 = (bf16[192,1024]{1,0:T(8,128)(2,1)S(1)}, bf16[192,1024]{1,0:T(8,128)(2,1)S(1)}, u32[]{:S(2)}, u32[]{:S(2)}) collective-permute-start(bf16[192,1024]{1,0:T(8,128)(2,1)S(1)} %convolution_convert_fusion.5), channel_id=1, source_target_pairs={{0,24},{8,16},{16,8},{24,0},{1,25},{9,17},{17,9},{25,1},{2,26},{10... | collective-permute-start | bytes 1179656 | tf_op jit(solution)/shard_map/ppermute | solution.py:141
Sparse Core Ops, SparseCore 0:
  19.6 62.0 reduce-scatter.4
  84.5 60.2 reduce-scatter.2
  162.5 34.6 all-gather.4
  198.6 35.8 all-gather.6
where the time goes:
time: 362 us; the launch traced here: 360 us
  waiting for transfers between devices  239 us (66%)
  matrix products  56.5 us (16%)
  local copies, waits for them, and re-layouts  19.1 us (5%)
  between operations  14 us (4%)
  starting transfers between devices  11 us (3%)
  blocking collectives  10.1 us (3%)
  other arithmetic  9.25 us (3%)
    ppermute x6, waiting for transfers between devices, on_device(): lax.ppermute(term, 'pass', perm)  66.7 us
    reduce_scatter x1, waiting for transfers between devices, on_device(): lax.psum_scatter(dense_partial, 'red', scatter_dimension=0, tiled=True)  63.2 us
    reduce_scatter x1, waiting for transfers between devices, on_device(): lax.psum_scatter(lex_partial, 'red', scatter_dimension=0, tiled=True)  56.5 us
    all_gather x1, waiting for transfers between devices, on_device(): lax.all_gather(grad_dense, 'red', axis=0, tiled=True)  27.9 us
    all_gather x1, waiting for transfers between devices, on_device(): lax.all_gather(grad_lex, 'red', axis=0, tiled=True)  24.8 us
    dot_general x2, matrix products, contract_rows(): lax.dot_general(first, second, (((1,), (1,)), ((), ())), preferred_elemen...  16.9 us
    dot_general x4, matrix products, query_terms(): jnp.dot(lax.dynamic_index_in_dim(chip_lex, place, 0, keepdims=False), chi...  15 us
    dot_general x2, matrix products, contract_columns(): lax.dot_general(first, second, (((0,), (0,)), ((), ())), preferred_elemen...  14.9 us
  transfers between devices with their start and end apart: 14, of which 6 were waited for; matrix products, arithmetic and copies ran while one was open for 16% of the time, Pallas kernels for 0%

commit v1 on v0

v1 whole, which is shorter than its diff:
```python
import functools

import jax
import jax.numpy as jnp
from jax import lax
from jax.experimental import pallas as pl
from jax.experimental.pallas import tpu as pltpu
from jax.sharding import PartitionSpec as P

MESH = pl.DeviceIdType.MESH
LANES = 128
STAT_ROWS = 16
F32 = jnp.float32
BF16 = jnp.bfloat16


class Plan:
    def __init__(self, query_lex, query_dense, passage_lex):
        self.red = lax.axis_size("red")
        self.passes = lax.axis_size("pass")
        self.cores = lax.axis_size("grp")
        self.queries, self.lex = query_lex.shape
        self.dense = query_dense.shape[1]
        self.passages = passage_lex.shape[0]
        self.block = self.queries // (self.passes * self.cores)
        self.rows = LANES // self.passes
        self.half = self.block // 2
        self.groups = self.half // self.rows
        self.chunks = self.groups * self.cores
        self.bits = self.passes.bit_length() - 1
        self.plane = self.passes * self.cores
        self.tile = min(512, self.lex, self.dense)
        self.columns = self.lex + self.dense
        tiles = self.columns // self.tile
        self.edges = [(s * tiles // self.bits) * self.tile for s in range(self.bits)] + [self.columns]
        self.keep_slots = -(-self.bits // self.cores)
        assert self.passes == 1 << self.bits and self.passes > 1
        assert self.groups * self.rows * 2 == self.block
        assert self.lex % self.tile == 0 and self.dense % self.tile == 0
        self.steps = self.chunks + 2 * (self.red - 1) + self.bits + 1


def fused(
    plan,
    ql_hbm, qd_hbm, pl_hbm, pd_hbm, pos_ref,
    g_out, loss_out, gql_out, gqd_out,
    qlv, qdv, plv, pdv, rs, grad, gx, st, lossb, tsend, trecv, keep,
    q_sem, p_sem, o_sem, ps_sem, pr_sem, rss_sem, rsr_sem, sts_sem, str_sem, gs_sem, gr_sem,
    xs_sem, xr_sem, ts_sem, tr_sem, ls_sem, lr_sem,
):
    n, passes, cores, chunks, bits = plan.red, plan.passes, plan.cores, plan.chunks, plan.bits
    me = lax.axis_index("red")
    my_pass = lax.axis_index("pass")
    my_core = lax.axis_index("grp")
    place = my_pass * cores + my_core
    hops = (n - 1 - me, me)
    onward = (me - 1, me + 1)
    back = (me + 1, me - 1)

    def local_q(d, c, t):
        core, group = lax.rem(c, cores), c // cores
        source = (ql_hbm, qd_hbm)[t]
        target = (qlv, qdv)[t]
        start = d * plan.half + group * plan.rows
        return pltpu.make_async_copy(
            source.at[:, core, pl.ds(pl.multiple_of(start, plan.rows), plan.rows), :],
            target.at[d, c],
            q_sem.at[d, c, t],
        )

    def local_p(t):
        return pltpu.make_async_copy((pl_hbm, pd_hbm)[t], (plv, pdv)[t].at[my_core], p_sem.at[t])

    def send_p(k, t):
        other = lax.rem(my_core + k, cores)
        return pltpu.make_async_remote_copy(
            src_ref=(pl_hbm, pd_hbm)[t],
            dst_ref=(plv, pdv)[t].at[my_core],
            send_sem=ps_sem.at[k - 1, t],
            recv_sem=pr_sem.at[k - 1, t],
            device_id={"grp": other},
            device_id_type=MESH,
        )

    def rs_copy(d, c, t):
        return pltpu.make_async_remote_copy(
            src_ref=rs.at[d, c, t],
            dst_ref=rs.at[d, c, t],
            send_sem=rss_sem.at[d, c, t],
            recv_sem=rsr_sem.at[d, c, t],
            device_id={"red": onward[d]},
            device_id_type=MESH,
        )

    def st_copy(c, k):
        peer = lax.rem(place + k, plan.plane)
        return pltpu.make_async_remote_copy(
            src_ref=st.at[c, place],
            dst_ref=st.at[c, place],
            send_sem=sts_sem.at[c, k - 1],
            recv_sem=str_sem.at[c, k - 1],
            device_id={"pass": peer // cores, "grp": lax.rem(peer, cores)},
            device_id_type=MESH,
        )

    def g_copy(d, c):
        return pltpu.make_async_remote_copy(
            src_ref=grad.at[d, c],
            dst_ref=grad.at[d, c],
            send_sem=gs_sem.at[d, c],
            recv_sem=gr_sem.at[d, c],
            device_id={"red": back[d]},
            device_id_type=MESH,
        )

    def g_store(d, c):
        return pltpu.make_async_copy(grad.at[d, c], g_out.at[d, c], o_sem.at[d, c])

    def x_copy(d, c, slot, target):
        return pltpu.make_async_remote_copy(
            src_ref=grad.at[d, c],
            dst_ref=gx.at[d, c // cores, slot],
            send_sem=xs_sem.at[d, c],
            recv_sem=xr_sem.at[d, c // cores, slot],
            device_id={"grp": target},
            device_id_type=MESH,
        )

    def part(phase):
        start = passes - (passes >> phase)
        return start, passes >> (phase + 1)

    def t_copy(d, group, phase, s):
        first, count = part(phase)
        lo, hi = plan.edges[s], plan.edges[s + 1]
        bit = (s + phase) % bits
        mine = lax.rem(my_pass // (1 << bit), 2)
        peer = my_pass + (1 - 2 * mine) * (1 << bit)
        where = (d, group, pl.ds(first, count), slice(None), pl.ds(lo, hi - lo))
        return pltpu.make_async_remote_copy(
            src_ref=tsend.at[where],
            dst_ref=trecv.at[where],
            send_sem=ts_sem.at[d, group, phase, s],
            recv_sem=tr_sem.at[d, group, phase, s],
            device_id={"pass": peer},
            device_id_type=MESH,
        )

    def loss_copy(d, k):
        return pltpu.make_async_remote_copy(
            src_ref=lossb.at[d],
            dst_ref=lossb.at[d],
            send_sem=ls_sem.at[k - 1],
            recv_sem=lr_sem.at[d],
            device_id={"red": lax.rem(me + k, n)},
            device_id_type=MESH,
        )

    for t in range(2):
        local_p(t).start()
    for c in range(chunks):
        for d in (1, 0):
            for t in range(2):
                local_q(d, c, t).start()

    barrier = pltpu.get_barrier_semaphore()
    for k in range(1, plan.plane):
        peer = lax.rem(place + k, plan.plane)
        pl.semaphore_signal(
            barrier, inc=1,
            device_id={"pass": peer // cores, "grp": lax.rem(peer, cores)}, device_id_type=MESH,
        )
    for k in range(1, n):
        pl.semaphore_signal(barrier, inc=1, device_id={"red": lax.rem(me + k, n)}, device_id_type=MESH)
    pl.semaphore_wait(barrier, plan.plane - 1 + n - 1)

    for k in range(1, cores):
        for t in range(2):
            send_p(k, t).start()
    for t in range(2):
        local_p(t).wait()

    first_column = place * plan.passages
    column = first_column + lax.broadcasted_iota(jnp.int32, (plan.passages, LANES), 0)

    def partial_scores(d, c, t):
        local_q(d, c, t).wait()
        rows = (qlv, qdv)[t][d, c].reshape(LANES, (plan.lex, plan.dense)[t])
        total = lax.dot_general(
            (plv, pdv)[t][my_core], rows, (((1,), (1,)), ((), ())), preferred_element_type=F32
        )
        rs_now = rs.at[d, c, t]

        @pl.when(hops[d] > 0)
        def _():
            rs_copy(d, c, t).wait_recv()
            rs_now[...] += total

        @pl.when(hops[d] == 0)
        def _():
            rs_now[...] = total

        @pl.when(hops[d] < n - 1)
        def _():
            rs_copy(d, c, t).start()

    def scores_of(d, c):
        lexical, dense = rs[d, c, 0], rs[d, c, 1]
        return dense + 0.3 * lexical, dense, lexical

    def statistics(d, c):
        scores = scores_of(d, c)
        joined, dense, lexical = scores
        target = column == pos_ref[d, c]
        st_now = st.at[c, place]
        powers = []
        for i in range(3):
            largest = jnp.max(scores[i], axis=0, keepdims=True)
            power = jnp.exp(scores[i] - largest)
            powers.append(power)
            st_now[i:i + 1] = largest
            st_now[3 + i:4 + i] = jnp.sum(power, axis=0, keepdims=True)
            st_now[8 + i:9 + i] = jnp.sum(jnp.where(target, scores[i], 0.0), axis=0, keepdims=True)
        st_now[6:7] = jnp.sum(powers[0] * (joined - dense), axis=0, keepdims=True)
        st_now[7:8] = jnp.sum(powers[0] * (joined - lexical), axis=0, keepdims=True)
        st_now[11:STAT_ROWS] = jnp.zeros((STAT_ROWS - 11, LANES), F32)
        for k in range(1, plan.plane):
            st_copy(c, k).start()

    def gradients(d, c):
        for k in range(1, plan.plane):
            st_copy(c, k).wait_recv()
        everyone = st[c]
        maxima = jnp.max(everyone[:, 0:3], axis=0)
        factors = jnp.exp(everyone[:, 0:3] - maxima[None])
        totals = jnp.sum(factors * everyone[:, 3:6], axis=0)
        weighted_dense = jnp.sum(factors[:, 0:1] * everyone[:, 6:7], axis=0)
        weighted_lex = jnp.sum(factors[:, 0:1] * everyone[:, 7:8], axis=0)
        picked = jnp.sum(everyone[:, 8:11], axis=0)
        logs = maxima + jnp.log(totals)
        log_joined, log_dense, log_lex = logs[0:1], logs[1:2], logs[2:3]
        kl_dense = weighted_dense / totals[0:1] - log_joined + log_dense
        kl_lex = weighted_lex / totals[0:1] - log_joined + log_lex
        loss = (
            log_joined - picked[0:1]
            + 0.5 * (log_dense - picked[1:2])
            + 0.5 * (log_lex - picked[2:3])
            + 0.5 * kl_dense
            + 0.5 * kl_lex
        )
        lossb[d, c] = jnp.broadcast_to(loss, (8, LANES))
        joined, dense, lexical = scores_of(d, c)
        target = (column == pos_ref[d, c]).astype(F32)
        prob = jnp.exp(joined - log_joined)
        grad[d, c, 0] = (-0.2 * prob + jnp.exp(lexical - log_lex) - 0.8 * target).astype(BF16)
        grad[d, c, 1] = (0.5 * prob + jnp.exp(dense - log_dense) - 1.5 * target).astype(BF16)

    def terms(d, c):
        group = c // cores
        slot = lax.rem(group, plan.keep_slots)
        for k in range(1, cores):
            x_copy(d, c, k - 1, lax.rem(my_core + k, cores)).wait_recv()
        for t in range(2):
            base = 0 if t == 0 else plan.lex
            lefts = [(my_core, grad[d, c, t].T)]
            for k in range(1, cores):
                lefts.append((lax.rem(my_core + k, cores), gx[d, group, k - 1, t].T))
            width = (plan.lex, plan.dense)[t]
            for s in range(bits):
                lo = max(plan.edges[s], base)
                hi = min(plan.edges[s + 1], base + width)
                if lo >= hi:
                    continue

                def column_tile(i, carry, lo=lo, s=s, t=t, base=base, lefts=lefts):
                    where = pl.ds(pl.multiple_of(lo - base + i * plan.tile, plan.tile), plan.tile)
                    there = pl.ds(pl.multiple_of(lo + i * plan.tile, plan.tile), plan.tile)
                    total = None
                    for core, left in lefts:
                        term = jnp.dot(left, (plv, pdv)[t][core, :, where], preferred_element_type=F32)
                        total = term if total is None else total + term
                    blocks = total.reshape(passes, plan.rows, plan.tile)
                    bit = s % bits
                    split = blocks.reshape(passes >> (bit + 1), 2, 1 << bit, plan.rows, plan.tile)
                    mine = lax.rem(my_pass // (1 << bit), 2)
                    zero, one = split[:, 0], split[:, 1]
                    pick = mine == 0
                    kept = jnp.where(pick, zero, one).reshape(passes // 2, plan.rows, plan.tile)
                    away = jnp.where(pick, one, zero).reshape(passes // 2, plan.rows, plan.tile)
                    first, count = part(0)
                    for a in range(count):
                        source = order(s, a)
                        tsend[d, group, first + a, :, there] = away[source].astype(BF16)
                        keep[d, slot, a, :, there] = kept[source]
                    return carry

                lax.fori_loop(0, (hi - lo) // plan.tile, column_tile, 0)
        for s in range(bits):
            t_copy(d, group, 0, s).start()

    def order(s, a):
        first_bit = s % bits
        natural = [bit for bit in range(bits) if bit != first_bit]
        place_of = 0
        for step in range(1, bits):
            bit = (s + step) % bits
            place_of |= ((a >> (step - 1)) & 1) << natural.index(bit)
        return place_of

    def later_phase(d, c, phase):
        group = c // cores
        slot = lax.rem(group, plan.keep_slots)
        for s in range(bits):
            t_copy(d, group, phase - 1, s).wait_recv()
            lo, hi = plan.edges[s], plan.edges[s + 1]
            before, had = part(phase - 1)
            first, count = part(phase)
            bit = (s + phase) % bits
            mine = lax.rem(my_pass // (1 << bit), 2)

            def column_tile(i, carry, lo=lo, before=before, first=first, count=count, mine=mine):
                there = pl.ds(pl.multiple_of(lo + i * plan.tile, plan.tile), plan.tile)
                for a in range(count):
                    both = []
                    for value in range(2):
                        b = 2 * a + value
                        both.append(keep[d, slot, b, :, there] + trecv[d, group, before + b, :, there].astype(F32))
                    pick = mine == 0
                    tsend[d, group, first + a, :, there] = jnp.where(pick, both[1], both[0]).astype(BF16)
                    keep[d, slot, a, :, there] = jnp.where(pick, both[0], both[1])
                return carry

            lax.fori_loop(0, (hi - lo) // plan.tile, column_tile, 0)
            t_copy(d, group, phase, s).start()

    def finish(d, c):
        group = c // cores
        slot = lax.rem(group, plan.keep_slots)
        last, _ = part(bits - 1)
        for s in range(bits):
            t_copy(d, group, bits - 1, s).wait_recv()
        for out, base, width in ((gql_out, 0, plan.lex), (gqd_out, plan.lex, plan.dense)):

            def column_tile(i, carry, out=out, base=base):
                there = pl.ds(pl.multiple_of(base + i * plan.tile, plan.tile), plan.tile)
                where = pl.ds(pl.multiple_of(i * plan.tile, plan.tile), plan.tile)
                out[d, group, :, where] = keep[d, slot, 0, :, there] + trecv[d, group, last, :, there].astype(F32)
                return carry

            lax.fori_loop(0, width // plan.tile, column_tile, 0)

    def inside(c):
        return jnp.logical_and(c >= 0, c < chunks)

    def step(tau, carry):
        for t in range(2):
            for d in range(2):
                c = tau - hops[d]

                @pl.when(inside(c))
                def _(d=d, c=c, t=t):
                    partial_scores(d, c, t)

        for d in range(2):
            c = tau - (n - 1)

            @pl.when(jnp.logical_and(inside(c), hops[d] == n - 1))
            def _(d=d, c=c):
                statistics(d, c)
                gradients(d, c)

                @pl.when(c == chunks - 1)
                def _():
                    for k in range(1, n):
                        loss_copy(d, k).start()

        for d in range(2):
            away = n - 1 - hops[d]
            c = tau - (n - 1) - away

            @pl.when(inside(c))
            def _(d=d, c=c, away=away):
                @pl.when(away > 0)
                def _():
                    g_copy(d, c).wait_recv()

                @pl.when(away < n - 1)
                def _():
                    g_copy(d, c).start()

                g_store(d, c).start()
                core = lax.rem(c, cores)

                @pl.when(core != my_core)
                def _():
                    x_copy(d, c, lax.rem(my_core - core + cores, cores) - 1, core).start()

        def my_turn(c):
            return jnp.logical_and(inside(c), lax.rem(c, cores) == my_core)

        for d in range(2):
            base = tau - (n - 1) - (n - 1 - hops[d])
            c = base - 1 - bits

            @pl.when(my_turn(c))
            def _(d=d, c=c):
                finish(d, c)

            for phase in range(bits - 1, 0, -1):
                c = base - 1 - phase

                @pl.when(my_turn(c))
                def _(d=d, c=c, phase=phase):
                    later_phase(d, c, phase)

            c = base - 1

            @pl.when(my_turn(c))
            def _(d=d, c=c):
                @pl.when(jnp.logical_and(c == my_core, d == first_half()))
                def _():
                    for k in range(1, cores):
                        for t in range(2):
                            send_p(k, t).wait_recv()

                terms(d, c)

        return carry

    def first_half():
        return jnp.where(hops[1] > hops[0], 1, 0)

    lax.fori_loop(0, plan.steps, step, 0)

    for d in range(2):
        @pl.when(hops[d] < n - 1)
        def _(d=d):
            pltpu.make_async_remote_copy(
                src_ref=lossb.at[d], dst_ref=lossb.at[d], send_sem=ls_sem.at[0], recv_sem=lr_sem.at[d],
                device_id={"red": lax.rem(me + 1, n)}, device_id_type=MESH,
            ).wait_recv()

        @pl.when(hops[d] == n - 1)
        def _(d=d):
            for k in range(1, n):
                loss_copy(d, k).wait_send()

        def drain(c, carry, d=d):
            g_store(d, c).wait()

            @pl.when(hops[d] < n - 1)
            def _():
                for t in range(2):
                    rs_copy(d, c, t).wait_send()

            @pl.when(hops[d] > 0)
            def _():
                g_copy(d, c).wait_send()

            @pl.when(hops[d] == n - 1)
            def _():
                for k in range(1, plan.plane):
                    st_copy(c, k).wait_send()

            core = lax.rem(c, cores)

            @pl.when(core != my_core)
            def _():
                x_copy(d, c, lax.rem(my_core - core + cores, cores) - 1, core).wait_send()

            @pl.when(core == my_core)
            def _():
                for phase in range(bits):
                    for s in range(bits):
                        t_copy(d, c // cores, phase, s).wait_send()

            return carry

        lax.fori_loop(0, chunks, drain, 0)
    for k in range(1, cores):
        for t in range(2):
            send_p(k, t).wait_send()
    loss_out[...] = lossb[...]


def on_device(query_lex, query_dense, passage_lex, passage_dense, positives):
    plan = Plan(query_lex, query_dense, passage_lex)
    n, passes, cores, chunks, groups, bits = plan.red, plan.passes, plan.cores, plan.chunks, plan.groups, plan.bits
    tiles = (passes, cores, 2, groups, plan.rows)
    pos = positives.reshape(tiles).transpose(2, 3, 1, 0, 4).reshape(2, chunks, 1, LANES)
    any_space = pl.BlockSpec(memory_space=pl.ANY)
    vmem = pl.BlockSpec(memory_space=pltpu.VMEM)
    dma = pltpu.SemaphoreType.DMA
    grads, loss, gql, gqd = pl.pallas_call(
        functools.partial(fused, plan),
        out_shape=(
            jax.ShapeDtypeStruct((2, chunks, 2, plan.passages, LANES), BF16),
            jax.ShapeDtypeStruct((2, chunks, 8, LANES), F32),
            jax.ShapeDtypeStruct((2, groups, plan.rows, plan.lex), F32),
            jax.ShapeDtypeStruct((2, groups, plan.rows, plan.dense), F32),
        ),
        in_specs=[any_space, any_space, any_space, any_space, vmem],
        out_specs=(any_space, vmem, vmem, vmem),
        scratch_shapes=[
            pltpu.VMEM((2, chunks, passes, plan.rows, plan.lex), BF16),
            pltpu.VMEM((2, chunks, passes, plan.rows, plan.dense), BF16),
            pltpu.VMEM((cores, plan.passages, plan.lex), BF16),
            pltpu.VMEM((cores, plan.passages, plan.dense), BF16),
            pltpu.VMEM((2, chunks, 2, plan.passages, LANES), F32),
            pltpu.VMEM((2, chunks, 2, plan.passages, LANES), BF16),
            pltpu.VMEM((2, groups, max(cores - 1, 1), 2, plan.passages, LANES), BF16),
            pltpu.VMEM((chunks, plan.plane, STAT_ROWS, LANES), F32),
            pltpu.VMEM((2, chunks, 8, LANES), F32),
            pltpu.VMEM((2, groups, passes - 1, plan.rows, plan.columns), BF16),
            pltpu.VMEM((2, groups, passes - 1, plan.rows, plan.columns), BF16),
            pltpu.VMEM((2, plan.keep_slots, passes // 2, plan.rows, plan.columns), F32),
            dma((2, chunks, 2)),
            dma((2,)),
            dma((2, chunks)),
            dma((max(cores - 1, 1), 2)),
            dma((max(cores - 1, 1), 2)),
            dma((2, chunks, 2)),
            dma((2, chunks, 2)),
            dma((chunks, plan.plane - 1)),
            dma((chunks, plan.plane - 1)),
            dma((2, chunks)),
            dma((2, chunks)),
            dma((2, chunks)),
            dma((2, groups, max(cores - 1, 1))),
            dma((2, groups, bits, bits)),
            dma((2, groups, bits, bits)),
            dma((max(n - 1, 1),)),
            dma((2,)),
        ],
        compiler_params=pltpu.CompilerParams(
            collective_id=0, has_side_effects=True, vmem_limit_bytes=67043328
        ),
    )(
        query_lex.reshape(passes, cores, plan.block, plan.lex),
        query_dense.reshape(passes, cores, plan.block, plan.dense),
        passage_lex,
        passage_dense,
        pos,
    )
    own_queries = plan.queries // n
    loss = loss[:, :, 0].reshape(2, groups, cores, passes, plan.rows).transpose(3, 2, 0, 1, 4).reshape(-1)
    loss_rows = lax.dynamic_slice_in_dim(loss, lax.axis_index("red") * own_queries, own_queries)
    whole = grads.reshape(2, groups, cores, 2, plan.passages, passes, plan.rows)
    whole = whole.transpose(3, 4, 5, 2, 0, 1, 6).reshape(2, plan.passages, plan.queries)
    grad_passage_lex = jnp.dot(whole[0], query_lex, preferred_element_type=F32)
    grad_passage_dense = jnp.dot(whole[1], query_dense, preferred_element_type=F32)
    return (
        loss_rows,
        gql.reshape(plan.block, plan.lex),
        gqd.reshape(plan.block, plan.dense),
        grad_passage_lex,
        grad_passage_dense,
    )


def solution(mesh):
    return jax.shard_map(
        on_device,
        mesh=mesh,
        in_specs=(
            P(None, "red"),
            P(None, "red"),
            P(("pass", "grp"), "red"),
            P(("pass", "grp"), "red"),
            P(),
        ),
        out_specs=(
            P("red"),
            P(("pass", "grp"), "red"),
            P(("pass", "grp"), "red"),
            P(("pass", "grp"), "red"),
            P(("pass", "grp"), "red"),
        ),
        check_vma=False,
    )
```

time: 362 us -> 201 us (0.56)
  waiting for transfers between devices: 239 us -> 0 us
  Pallas kernels: 0 us -> 176 us
  matrix products: 56.5 us -> 12.3 us
  between operations: 14 us -> 0.73 us
  starting transfers between devices: 11 us -> 0 us
  blocking collectives: 10.1 us -> 0 us
  other arithmetic: 9.25 us -> 0.01 us
  local copies, waits for them, and re-layouts: 19.1 us -> 12.3 us
    pallas_call x0 -> x1, Pallas kernels: none -> 176 us  [on_device(): pl.pallas_call(functools.partial(fused, plan), out_shape=(jax.ShapeDtypeS...]
    reduce_scatter x2 -> x0, waiting for transfers between devices: 120 us -> none  [the longest x1 63.2 us: on_device(): lax.psum_scatter(dense_partial, 'red', scatter_dimension=0, tiled=True)]
    ppermute x10 -> x0, waiting for transfers between devices: 66.7 us -> none  [the longest x6 66.7 us: on_device(): lax.ppermute(term, 'pass', perm)]
    all_gather x2 -> x0, waiting for transfers between devices: 52.6 us -> none  [the longest x1 27.9 us: on_device(): lax.all_gather(grad_dense, 'red', axis=0, tiled=True)]
    dot_general x12 -> x2, matrix products: 56.5 us -> 12.3 us  [the longest x1 9.19 us: on_device(): grad_passage_lex = jnp.dot(whole[0], query_lex, preferred_element_type=F32)]
    ppermute x10 -> x0, starting transfers between devices: 10.7 us -> none  [the longest x6 7.21 us: on_device(): lax.ppermute(term, 'pass', perm)]
    all_gather x1 -> x0, blocking collectives: 10.1 us -> none  [on_device(): everyone = lax.all_gather(stats, ('pass', 'grp'), axis=0)]
    concatenate x2 -> x0, local copies, waits for them, and re-layouts: 6.96 us -> none  [from_chip(): return jnp.concatenate(pieces, axis=0)]
  transfers between devices with their start and end apart: 14 -> 0, of which waited for: 6 -> 0; matrix products, arithmetic and copies ran while one was open for 16% -> 0% of each run, Pallas kernels for 0% -> 0%
where the time goes in v1:
time: 201 us
  Pallas kernels  176 us (88%)
  local copies, waits for them, and re-layouts  12.3 us (6%)
  matrix products  12.3 us (6%)
    pallas_call x1, Pallas kernels, on_device(): pl.pallas_call(functools.partial(fused, plan), out_shape=(jax.ShapeDtypeS...  176 us
    dot_general x1, matrix products, on_device(): grad_passage_lex = jnp.dot(whole[0], query_lex, preferred_element_type=F32)  9.19 us
    unnamed x14, local copies, waits for them, and re-layouts  5.45 us

profile of v1, /device:TPU:1, one launch (start us, length us, event | category | flops | bytes accessed | tf_op | source)
XLA Modules:
  0.0 200.9 jit_solution(8558320930265963941)
XLA Ops:
  0.6 0.8 reshape.41
  1.4 0.7 reshape.42.pos_ref
  2.1 175.6 %shard_map.92 = (bf16[2,6,2,512,128]{4,3,2,1,0:T(8,128)(2,1)}, f32[2,6,8,128]{3,2,1,0:T(8,128)}, f32[2,3,32,4096]{3,2,1,0:T(8,128)}, f32[2,3,32,1024]{3,2,1,0:T(8,128)}) custom-call(bf16[4,2,192,4096]{3,2,1,0:T(8,128)(2,1)} %bitcast.17, bf16[4,2,192,1024]{3,2,1,0:T(8,128)(2,1)} %bitcast.21, bf16[512,4096]{1,0:T(8,128)(2,1)} %pl_hbm.1, ...), custom_call_target="tpu_custom_call" | custom-call | tf_op jit(solution)/shard_map/pallas_call | solution.py:494
  177.7 0.8 slice_reduce_fusion
  178.6 0.1 reshape_squeeze.3
  178.7 0.1 reshape.43
  178.7 0.7 dynamic_slice.3
  179.4 3.2 %copy.12 = bf16[2,6,2,512,128]{3,4,2,1,0:T(8,128)(2,1)S(1)} copy(bf16[2,6,2,512,128]{4,3,2,1,0:T(8,128)(2,1)} %get-tuple-element.12) | data formatting | bytes 6291456 | tf_op jit(solution)/shard_map/pallas_call | solution.py:494
  182.6 0.0 slice-start
  182.6 0.2 fusion
  182.8 0.0 copy-start
  182.8 0.0 slice-start.1
  182.9 0.2 copy.14
  183.0 1.8 copy-done
  184.9 0.0 slice-start.2
  184.9 3.1 %fusion.2 = f32[512,1024]{1,0:T(8,128)} fusion(bf16[512,1536]{0,1:T(8,128)(2,1)S(1)} %bitcast.23, bf16[1536,1024]{1,0:T(8,128)(2,1)S(1)} %copy-done), kind=kOutput, calls=%fused_computation.4 | convolution fusion | flops 1610612736 | bytes 6815744 | tf_op jit(solution)/shard_map/dot_general | solution.py:551
  188.0 0.1 copy.13
  188.1 0.0 slice-done
  188.1 0.0 slice-done.1
  188.1 1.0 slice-done.2
  189.2 0.0 copy-start.1
  189.2 9.2 %fusion.1 = f32[512,4096]{1,0:T(8,128)} fusion(bf16[512,1536]{0,1:T(8,128)(2,1)S(1)} %bitcast.24, bf16[1536,4096]{1,0:T(8,128)(2,1)S(1)} %bitcast.19), kind=kOutput, calls=%fused_computation.3 | convolution fusion | flops 6442450944 | bytes 22544384 | tf_op jit(solution)/shard_map/dot_general | solution.py:550
  198.4 0.0 copy-done.1
  198.4 0.0 copy-start.2
  198.4 1.7 copy.19
  200.0 0.0 copy-done.2
  200.0 0.9 copy.20
  (3 shorter events, 0.0 us)
Async XLA Ops:
  182.6 5.5 %slice-start = ((s8[12582912]{0:T(1024)(128)(4,1)}), s8[4194304]{0:T(1024)(128)(4,1)S(1)}, s32[]{:S(2)}) async-start(s8[12582912]{0:T(1024)(128)(4,1)} %bitcast.18), calls=%async_computation | async-start | bytes 8388608
  182.8 2.0 %copy-start = (bf16[1536,1024]{1,0:T(8,128)(2,1)S(1)}, bf16[1536,1024]{1,0:T(8,128)(2,1)}, u32[]{:S(2)}) copy-start(bf16[1536,1024]{1,0:T(8,128)(2,1)} %param.6) | copy-start | bytes 9437188
  182.8 5.3 %slice-start.1 = ((s8[12582912]{0:T(1024)(128)(4,1)}), s8[4194304]{0:T(1024)(128)(4,1)S(1)}, s32[]{:S(2)}) async-start(s8[12582912]{0:T(1024)(128)(4,1)} %bitcast.18), calls=%async_computation.1 | async-start | bytes 8388608
  184.9 4.3 %slice-start.2 = ((s8[12582912]{0:T(1024)(128)(4,1)}), s8[4194304]{0:T(1024)(128)(4,1)S(1)}, s32[]{:S(2)}) async-start(s8[12582912]{0:T(1024)(128)(4,1)} %bitcast.18), calls=%async_computation.2 | async-start | bytes 8388608
  189.2 9.2 %copy-start.1 = (f32[2,3,32,4096]{3,2,1,0:T(8,128)S(1)}, f32[2,3,32,4096]{3,2,1,0:T(8,128)}, u32[]{:S(2)}) copy-start(f32[2,3,32,4096]{3,2,1,0:T(8,128)} %get-tuple-element.10) | copy-start | bytes 9437188
  198.4 1.7 copy-start.2

commit v2 on v1

--- a/solution.py
+++ b/solution.py
@@ -9,7 +9,8 @@
 
 MESH = pl.DeviceIdType.MESH
 LANES = 128
-STAT_ROWS = 16
+HALF = LANES // 2
+STAT_ROWS = 8
 F32 = jnp.float32
 BF16 = jnp.bfloat16
 
@@ -26,29 +27,33 @@
         self.rows = LANES // self.passes
         self.half = self.block // 2
         self.groups = self.half // self.rows
-        self.chunks = self.groups * self.cores
+        self.pairs = self.groups * self.cores
+        self.chunks = 2 * self.pairs
         self.bits = self.passes.bit_length() - 1
         self.plane = self.passes * self.cores
         self.tile = min(512, self.lex, self.dense)
         self.columns = self.lex + self.dense
         tiles = self.columns // self.tile
         self.edges = [(s * tiles // self.bits) * self.tile for s in range(self.bits)] + [self.columns]
-        self.keep_slots = -(-self.bits // self.cores)
+        self.lag = 2
+        self.keep_slots = -(-self.bits * self.lag // (2 * self.cores))
+        self.parts = 2
         assert self.passes == 1 << self.bits and self.passes > 1
         assert self.groups * self.rows * 2 == self.block
         assert self.lex % self.tile == 0 and self.dense % self.tile == 0
-        self.steps = self.chunks + 2 * (self.red - 1) + self.bits + 1
+        self.steps = self.chunks + 2 * self.red + self.bits * self.lag
 
 
 def fused(
     plan,
     ql_hbm, qd_hbm, pl_hbm, pd_hbm, pos_ref,
-    g_out, loss_out, gql_out, gqd_out,
-    qlv, qdv, plv, pdv, rs, grad, gx, st, lossb, tsend, trecv, keep,
-    q_sem, p_sem, o_sem, ps_sem, pr_sem, rss_sem, rsr_sem, sts_sem, str_sem, gs_sem, gr_sem,
+    loss_out, gql_out, gqd_out, left_out, qlp_out, qdp_out,
+    qlv, qdv, plv, pdv, rs, own, grad, left, gx, st, lossb, tsend, trecv, keep,
+    q_sem, p_sem, o_sem, w_sem, ps_sem, pr_sem, rss_sem, rsr_sem, sts_sem, str_sem, gs_sem, gr_sem,
     xs_sem, xr_sem, ts_sem, tr_sem, ls_sem, lr_sem,
 ):
     n, passes, cores, chunks, bits = plan.red, plan.passes, plan.cores, plan.chunks, plan.bits
+    pairs = plan.pairs
     me = lax.axis_index("red")
     my_pass = lax.axis_index("pass")
     my_core = lax.axis_index("grp")
@@ -82,12 +87,14 @@
             device_id_type=MESH,
         )
 
-    def rs_copy(d, c, t):
+    def rs_copy(d, u, part):
+        size = plan.passages // plan.parts
+        where = (d, u, pl.ds(part * size, size))
         return pltpu.make_async_remote_copy(
-            src_ref=rs.at[d, c, t],
-            dst_ref=rs.at[d, c, t],
-            send_sem=rss_sem.at[d, c, t],
-            recv_sem=rsr_sem.at[d, c, t],
+            src_ref=rs.at[where],
+            dst_ref=rs.at[where],
+            send_sem=rss_sem.at[d, u, part],
+            recv_sem=rsr_sem.at[d, u, part],
             device_id={"red": onward[d]},
             device_id_type=MESH,
         )
@@ -113,15 +120,20 @@
             device_id_type=MESH,
         )
 
-    def g_store(d, c):
-        return pltpu.make_async_copy(grad.at[d, c], g_out.at[d, c], o_sem.at[d, c])
-
-    def x_copy(d, c, slot, target):
+    def left_store(d, c):
+        where = pl.ds(pl.multiple_of((d * pairs + c) * LANES, LANES), LANES)
+        return pltpu.make_async_copy(left.at[:, :, where], left_out.at[:, :, where], o_sem.at[d, c])
+
+    def q_store(d, c, t):
+        return pltpu.make_async_copy((qlv, qdv)[t].at[d, c], (qlp_out, qdp_out)[t].at[d, c], w_sem.at[d, c, t])
+
+    def x_copy(d, u, slot, target):
+        group = u // (2 * cores)
         return pltpu.make_async_remote_copy(
-            src_ref=grad.at[d, c],
-            dst_ref=gx.at[d, c // cores, slot],
-            send_sem=xs_sem.at[d, c],
-            recv_sem=xr_sem.at[d, c // cores, slot],
+            src_ref=grad.at[d, u],
+            dst_ref=gx.at[d, group, lax.rem(u, 2), slot],
+            send_sem=xs_sem.at[d, u],
+            recv_sem=xr_sem.at[d, group, lax.rem(u, 2), slot],
             device_id={"grp": target},
             device_id_type=MESH,
         )
@@ -158,10 +170,9 @@
 
     for t in range(2):
         local_p(t).start()
-    for c in range(chunks):
-        for d in (1, 0):
-            for t in range(2):
-                local_q(d, c, t).start()
+    for d in range(2):
+        for t in range(2):
+            local_q(d, 0, t).start()
 
     barrier = pltpu.get_barrier_semaphore()
     for k in range(1, plan.plane):
@@ -174,97 +185,116 @@
         pl.semaphore_signal(barrier, inc=1, device_id={"red": lax.rem(me + k, n)}, device_id_type=MESH)
     pl.semaphore_wait(barrier, plan.plane - 1 + n - 1)
 
+    for t in range(2):
+        local_p(t).wait()
+    for c in range(1, pairs):
+        for d in range(2):
+            for t in range(2):
+                local_q(d, c, t).start()
     for k in range(1, cores):
         for t in range(2):
             send_p(k, t).start()
-    for t in range(2):
-        local_p(t).wait()
 
     first_column = place * plan.passages
     column = first_column + lax.broadcasted_iota(jnp.int32, (plan.passages, LANES), 0)
 
-    def partial_scores(d, c, t):
-        local_q(d, c, t).wait()
-        rows = (qlv, qdv)[t][d, c].reshape(LANES, (plan.lex, plan.dense)[t])
-        total = lax.dot_general(
-            (plv, pdv)[t][my_core], rows, (((1,), (1,)), ((), ())), preferred_element_type=F32
-        )
-        rs_now = rs.at[d, c, t]
+    low = lax.broadcasted_iota(jnp.int32, (plan.passages, LANES), 1) < HALF
+    low_row = lax.broadcasted_iota(jnp.int32, (1, LANES), 1) < HALF
+
+    def swap(values):
+        return pltpu.roll(values, HALF, 1)
+
+    def own_scores(d, c):
+        totals = []
+        for t in range(2):
+            local_q(d, c, t).wait()
+            q_store(d, c, t).start()
+            rows = (qlv, qdv)[t][d, c].reshape(LANES, (plan.lex, plan.dense)[t])
+            totals.append(lax.dot_general(
+                (plv, pdv)[t][my_core], rows, (((1,), (1,)), ((), ())), preferred_element_type=F32
+            ))
+        lexical, dense = totals
+        own[d, 0] = jnp.where(low, lexical, swap(dense))
+        own[d, 1] = jnp.where(low, swap(lexical), dense)
+
+    def add_scores(d, u, part):
+        size = plan.passages // plan.parts
+        where = pl.ds(part * size, size)
+        mine = own.at[d, lax.rem(u, 2), where]
+        rs_now = rs.at[d, u, where]
 
         @pl.when(hops[d] > 0)
         def _():
-            rs_copy(d, c, t).wait_recv()
-            rs_now[...] += total
+            rs_copy(d, u, part).wait_recv()
+            rs_now[...] += mine[...]
 
         @pl.when(hops[d] == 0)
         def _():
-            rs_now[...] = total
+            rs_now[...] = mine[...]
 
         @pl.when(hops[d] < n - 1)
         def _():
-            rs_copy(d, c, t).start()
-
-    def scores_of(d, c):
-        lexical, dense = rs[d, c, 0], rs[d, c, 1]
-        return dense + 0.3 * lexical, dense, lexical
-
-    def statistics(d, c):
-        scores = scores_of(d, c)
-        joined, dense, lexical = scores
-        target = column == pos_ref[d, c]
-        st_now = st.at[c, place]
-        powers = []
-        for i in range(3):
-            largest = jnp.max(scores[i], axis=0, keepdims=True)
-            power = jnp.exp(scores[i] - largest)
-            powers.append(power)
-            st_now[i:i + 1] = largest
-            st_now[3 + i:4 + i] = jnp.sum(power, axis=0, keepdims=True)
-            st_now[8 + i:9 + i] = jnp.sum(jnp.where(target, scores[i], 0.0), axis=0, keepdims=True)
-        st_now[6:7] = jnp.sum(powers[0] * (joined - dense), axis=0, keepdims=True)
-        st_now[7:8] = jnp.sum(powers[0] * (joined - lexical), axis=0, keepdims=True)
-        st_now[11:STAT_ROWS] = jnp.zeros((STAT_ROWS - 11, LANES), F32)
+            rs_copy(d, u, part).start()
+
+    def joined_of(scores):
+        other = swap(scores)
+        return jnp.where(low, other + 0.3 * scores, scores + 0.3 * other)
+
+    def statistics(d, u):
+        scores = rs[d, u]
+        joined = joined_of(scores)
+        target = column == pos_ref[d, u]
+        st_now = st.at[u, place]
+        largest = jnp.max(scores, axis=0, keepdims=True)
+        largest_joined = jnp.max(joined, axis=0, keepdims=True)
+        power = jnp.exp(joined - largest_joined)
+        st_now[0:1] = largest
+        st_now[1:2] = largest_joined
+        st_now[2:3] = jnp.sum(jnp.exp(scores - largest), axis=0, keepdims=True)
+        st_now[3:4] = jnp.sum(power, axis=0, keepdims=True)
+        st_now[4:5] = jnp.sum(power * (joined - scores), axis=0, keepdims=True)
+        st_now[5:6] = jnp.sum(jnp.where(target, scores, 0.0), axis=0, keepdims=True)
+        st_now[6:7] = jnp.sum(jnp.where(target, joined, 0.0), axis=0, keepdims=True)
+        st_now[7:8] = jnp.zeros((1, LANES), F32)
         for k in range(1, plan.plane):
-            st_copy(c, k).start()
-
-    def gradients(d, c):
+            st_copy(u, k).start()
+
+    def gradients(d, u):
         for k in range(1, plan.plane):
-            st_copy(c, k).wait_recv()
-        everyone = st[c]
-        maxima = jnp.max(everyone[:, 0:3], axis=0)
-        factors = jnp.exp(everyone[:, 0:3] - maxima[None])
-        totals = jnp.sum(factors * everyone[:, 3:6], axis=0)
-        weighted_dense = jnp.sum(factors[:, 0:1] * everyone[:, 6:7], axis=0)
-        weighted_lex = jnp.sum(factors[:, 0:1] * everyone[:, 7:8], axis=0)
-        picked = jnp.sum(everyone[:, 8:11], axis=0)
+            st_copy(u, k).wait_recv()
+        everyone = st[u]
+        maxima = jnp.max(everyone[:, 0:2], axis=0)
+        factors = jnp.exp(everyone[:, 0:2] - maxima[None])
+        totals = jnp.sum(factors * everyone[:, 2:4], axis=0)
+        weighted = jnp.sum(factors[:, 1:2] * everyone[:, 4:5], axis=0)
+        picked = jnp.sum(everyone[:, 5:7], axis=0)
         logs = maxima + jnp.log(totals)
-        log_joined, log_dense, log_lex = logs[0:1], logs[1:2], logs[2:3]
-        kl_dense = weighted_dense / totals[0:1] - log_joined + log_dense
-        kl_lex = weighted_lex / totals[0:1] - log_joined + log_lex
-        loss = (
-            log_joined - picked[0:1]
-            + 0.5 * (log_dense - picked[1:2])
-            + 0.5 * (log_lex - picked[2:3])
-            + 0.5 * kl_dense
-            + 0.5 * kl_lex
-        )
-        lossb[d, c] = jnp.broadcast_to(loss, (8, LANES))
-        joined, dense, lexical = scores_of(d, c)
-        target = (column == pos_ref[d, c]).astype(F32)
-        prob = jnp.exp(joined - log_joined)
-        grad[d, c, 0] = (-0.2 * prob + jnp.exp(lexical - log_lex) - 0.8 * target).astype(BF16)
-        grad[d, c, 1] = (0.5 * prob + jnp.exp(dense - log_dense) - 1.5 * target).astype(BF16)
+        log_own, log_joined = logs[0:1], logs[1:2]
+        divergence = weighted / totals[1:2] - log_joined + log_own
+        share = 0.5 * (log_own - picked[0:1]) + 0.5 * divergence
+        loss = (log_joined - picked[1:2]) + (share + swap(share))
+        lossb[d, u] = jnp.broadcast_to(loss, (8, LANES))
+        scores = rs[d, u]
+        joined = joined_of(scores)
+        prob = jnp.where(low_row, -0.2, 0.5) * jnp.exp(joined - log_joined) + jnp.exp(scores - log_own)
+        hit = jnp.where(column == pos_ref[d, u], jnp.where(low_row, 0.8, 1.5), 0.0)
+        grad[d, u] = (prob - hit).astype(BF16)
 
     def terms(d, c):
         group = c // cores
         slot = lax.rem(group, plan.keep_slots)
+        turned = [(my_core, [grad[d, 2 * c + h].T for h in range(2)])]
         for k in range(1, cores):
-            x_copy(d, c, k - 1, lax.rem(my_core + k, cores)).wait_recv()
+            core = lax.rem(my_core + k, cores)
+            for h in range(2):
+                x_copy(d, 2 * c + h, k - 1, core).wait_recv()
+            turned.append((core, [gx[d, group, h, k - 1].T for h in range(2)]))
         for t in range(2):
             base = 0 if t == 0 else plan.lex
-            lefts = [(my_core, grad[d, c, t].T)]
-            for k in range(1, cores):
-                lefts.append((lax.rem(my_core + k, cores), gx[d, group, k - 1, t].T))
+            lefts = [
+                (core, jnp.concatenate([half[t * HALF:(t + 1) * HALF] for half in halves], axis=0))
+                for core, halves in turned
+            ]
             width = (plan.lex, plan.dense)[t]
             for s in range(bits):
                 lo = max(plan.edges[s], base)
@@ -349,74 +379,41 @@
 
             lax.fori_loop(0, width // plan.tile, column_tile, 0)
 
-    def inside(c):
-        return jnp.logical_and(c >= 0, c < chunks)
+    def lay_out(d, c):
+        halves = [grad[d, 2 * c + h].astype(F32) for h in range(2)]
+        where = pl.ds(pl.multiple_of((d * pairs + c) * LANES, LANES), LANES)
+        left[0, :, where] = jnp.where(low, halves[0], swap(halves[1])).astype(BF16)
+        left[1, :, where] = jnp.where(low, swap(halves[0]), halves[1]).astype(BF16)
+        left_store(d, c).start()
+
+    def inside(u):
+        return jnp.logical_and(u >= 0, u < chunks)
 
     def step(tau, carry):
-        for t in range(2):
-            for d in range(2):
-                c = tau - hops[d]
-
-                @pl.when(inside(c))
-                def _(d=d, c=c, t=t):
-                    partial_scores(d, c, t)
+        def my_turn(u):
+            return jnp.logical_and(
+                inside(u), jnp.logical_and(lax.rem(u, 2) == 1, lax.rem(u // 2, cores) == my_core)
+            )
 
         for d in range(2):
-            c = tau - (n - 1)
-
-            @pl.when(jnp.logical_and(inside(c), hops[d] == n - 1))
-            def _(d=d, c=c):
-                statistics(d, c)
-                gradients(d, c)
-
-                @pl.when(c == chunks - 1)
-                def _():
-                    for k in range(1, n):
-                        loss_copy(d, k).start()
-
-        for d in range(2):
-            away = n - 1 - hops[d]
-            c = tau - (n - 1) - away
-
-            @pl.when(inside(c))
-            def _(d=d, c=c, away=away):
-                @pl.when(away > 0)
-                def _():
-                    g_copy(d, c).wait_recv()
-
-                @pl.when(away < n - 1)
-                def _():
-                    g_copy(d, c).start()
-
-                g_store(d, c).start()
-                core = lax.rem(c, cores)
-
-                @pl.when(core != my_core)
-                def _():
-                    x_copy(d, c, lax.rem(my_core - core + cores, cores) - 1, core).start()
-
-        def my_turn(c):
-            return jnp.logical_and(inside(c), lax.rem(c, cores) == my_core)
-
-        for d in range(2):
-            base = tau - (n - 1) - (n - 1 - hops[d])
-            c = base - 1 - bits
-
-            @pl.when(my_turn(c))
-            def _(d=d, c=c):
-                finish(d, c)
+            base = tau - (n - 1) - 2 - (n - 1 - hops[d])
+            u = base - plan.lag * bits
+
+            @pl.when(my_turn(u))
+            def _(d=d, u=u):
+                finish(d, u // 2)
 
             for phase in range(bits - 1, 0, -1):
-                c = base - 1 - phase
-
-                @pl.when(my_turn(c))
-                def _(d=d, c=c, phase=phase):
-                    later_phase(d, c, phase)
-
-            c = base - 1
-
-            @pl.when(my_turn(c))
-            def _(d=d, c=c):
+                u = base - plan.lag * phase
+
+                @pl.when(my_turn(u))
+                def _(d=d, u=u, phase=phase):
+                    later_phase(d, u // 2, phase)
+
+            @pl.when(my_turn(base))
+            def _(d=d, u=base):
+                c = u // 2
+
                 @pl.when(jnp.logical_and(c == my_core, d == first_half()))
                 def _():
                     for k in range(1, cores):
@@ -424,6 +421,61 @@
                             send_p(k, t).wait_recv()
 
                 terms(d, c)
+
+        for part in range(plan.parts):
+            for d in range(2):
+                u = tau - hops[d]
+                if part == 0:
+                    @pl.when(jnp.logical_and(inside(u), lax.rem(u, 2) == 0))
+                    def _(d=d, u=u):
+                        own_scores(d, u // 2)
+
+                @pl.when(inside(u))
+                def _(d=d, u=u, part=part):
+                    add_scores(d, u, part)
+
+        for d in range(2):
+            u = tau - (n - 1) - 1
+
+            @pl.when(jnp.logical_and(inside(u), hops[d] == n - 1))
+            def _(d=d, u=u):
+                gradients(d, u)
+
+                @pl.when(u == chunks - 1)
+                def _():
+                    for k in range(1, n):
+                        loss_copy(d, k).start()
+
+        for d in range(2):
+            u = tau - (n - 1)
+
+            @pl.when(jnp.logical_and(inside(u), hops[d] == n - 1))
+            def _(d=d, u=u):
+                statistics(d, u)
+
+        for d in range(2):
+            away = n - 1 - hops[d]
+            u = tau - (n - 1) - 1 - away
+
+            @pl.when(inside(u))
+            def _(d=d, u=u, away=away):
+                @pl.when(away > 0)
+                def _():
+                    g_copy(d, u).wait_recv()
+
+                @pl.when(away < n - 1)
+                def _():
+                    g_copy(d, u).start()
+
+                core = lax.rem(u // 2, cores)
+
+                @pl.when(core != my_core)
+                def _():
+                    x_copy(d, u, lax.rem(my_core - core + cores, cores) - 1, core).start()
+
+                @pl.when(lax.rem(u, 2) == 1)
+                def _():
+                    lay_out(d, u // 2)
 
         return carry
 
@@ -446,12 +498,10 @@
                 loss_copy(d, k).wait_send()
 
         def drain(c, carry, d=d):
-            g_store(d, c).wait()
-
             @pl.when(hops[d] < n - 1)
             def _():
-                for t in range(2):
-                    rs_copy(d, c, t).wait_send()
+                for part in range(plan.parts):
+                    rs_copy(d, c, part).wait_send()
 
             @pl.when(hops[d] > 0)
             def _():
@@ -462,17 +512,17 @@
                 for k in range(1, plan.plane):
                     st_copy(c, k).wait_send()
 
-            core = lax.rem(c, cores)
+            core = lax.rem(c // 2, cores)
 
             @pl.when(core != my_core)
             def _():
                 x_copy(d, c, lax.rem(my_core - core + cores, cores) - 1, core).wait_send()
 
-            @pl.when(core == my_core)
+            @pl.when(jnp.logical_and(core == my_core, lax.rem(c, 2) == 1))
             def _():
                 for phase in range(bits):
                     for s in range(bits):
-                        t_copy(d, c // cores, phase, s).wait_send()
+                        t_copy(d, c // (2 * cores), phase, s).wait_send()
 
             return carry
 
@@ -480,53 +530,66 @@
     for k in range(1, cores):
         for t in range(2):
             send_p(k, t).wait_send()
+    for d in range(2):
+        for c in range(pairs):
+            left_store(d, c).wait()
+            for t in range(2):
+                q_store(d, c, t).wait()
     loss_out[...] = lossb[...]
 
 
 def on_device(query_lex, query_dense, passage_lex, passage_dense, positives):
     plan = Plan(query_lex, query_dense, passage_lex)
     n, passes, cores, chunks, groups, bits = plan.red, plan.passes, plan.cores, plan.chunks, plan.groups, plan.bits
-    tiles = (passes, cores, 2, groups, plan.rows)
-    pos = positives.reshape(tiles).transpose(2, 3, 1, 0, 4).reshape(2, chunks, 1, LANES)
+    pos = positives.reshape(passes, cores, 2, groups, plan.rows).transpose(2, 3, 1, 0, 4).reshape(2, chunks, 1, HALF)
+    pos = jnp.concatenate([pos, pos], axis=-1)
     any_space = pl.BlockSpec(memory_space=pl.ANY)
     vmem = pl.BlockSpec(memory_space=pltpu.VMEM)
     dma = pltpu.SemaphoreType.DMA
-    grads, loss, gql, gqd = pl.pallas_call(
+    others = max(cores - 1, 1)
+    lex_rows = query_lex.reshape(passes, cores, plan.block, plan.lex)
+    dense_rows = query_dense.reshape(passes, cores, plan.block, plan.dense)
+    loss, gql, gqd, left, lex_ordered, dense_ordered = pl.pallas_call(
         functools.partial(fused, plan),
         out_shape=(
-            jax.ShapeDtypeStruct((2, chunks, 2, plan.passages, LANES), BF16),
             jax.ShapeDtypeStruct((2, chunks, 8, LANES), F32),
             jax.ShapeDtypeStruct((2, groups, plan.rows, plan.lex), F32),
             jax.ShapeDtypeStruct((2, groups, plan.rows, plan.dense), F32),
+            jax.ShapeDtypeStruct((2, plan.passages, plan.queries), BF16),
+            jax.ShapeDtypeStruct((2, plan.pairs, passes, plan.rows, plan.lex), BF16),
+            jax.ShapeDtypeStruct((2, plan.pairs, passes, plan.rows, plan.dense), BF16),
         ),
         in_specs=[any_space, any_space, any_space, any_space, vmem],
-        out_specs=(any_space, vmem, vmem, vmem),
+        out_specs=(vmem, vmem, vmem, any_space, any_space, any_space),
         scratch_shapes=[
-            pltpu.VMEM((2, chunks, passes, plan.rows, plan.lex), BF16),
-            pltpu.VMEM((2, chunks, passes, plan.rows, plan.dense), BF16),
+            pltpu.VMEM((2, plan.pairs, passes, plan.rows, plan.lex), BF16),
+            pltpu.VMEM((2, plan.pairs, passes, plan.rows, plan.dense), BF16),
             pltpu.VMEM((cores, plan.passages, plan.lex), BF16),
             pltpu.VMEM((cores, plan.passages, plan.dense), BF16),
-            pltpu.VMEM((2, chunks, 2, plan.passages, LANES), F32),
-            pltpu.VMEM((2, chunks, 2, plan.passages, LANES), BF16),
-            pltpu.VMEM((2, groups, max(cores - 1, 1), 2, plan.passages, LANES), BF16),
+            pltpu.VMEM((2, chunks, plan.passages, LANES), F32),
+            pltpu.VMEM((2, 2, plan.passages, LANES), F32),
+            pltpu.VMEM((2, chunks, plan.passages, LANES), BF16),
+            pltpu.VMEM((2, plan.passages, plan.queries), BF16),
+            pltpu.VMEM((2, groups, 2, others, plan.passages, LANES), BF16),
             pltpu.VMEM((chunks, plan.plane, STAT_ROWS, LANES), F32),
             pltpu.VMEM((2, chunks, 8, LANES), F32),
             pltpu.VMEM((2, groups, passes - 1, plan.rows, plan.columns), BF16),
             pltpu.VMEM((2, groups, passes - 1, plan.rows, plan.columns), BF16),
             pltpu.VMEM((2, plan.keep_slots, passes // 2, plan.rows, plan.columns), F32),
-            dma((2, chunks, 2)),
+            dma((2, plan.pairs, 2)),
             dma((2,)),
-            dma((2, chunks)),
-            dma((max(cores - 1, 1), 2)),
-            dma((max(cores - 1, 1), 2)),
-            dma((2, chunks, 2)),
-            dma((2, chunks, 2)),
+            dma((2, plan.pairs)),
+            dma((2, plan.pairs, 2)),
+            dma((others, 2)),
+            dma((others, 2)),
+            dma((2, chunks, plan.parts)),
+            dma((2, chunks, plan.parts)),
             dma((chunks, plan.plane - 1)),
             dma((chunks, plan.plane - 1)),
             dma((2, chunks)),
             dma((2, chunks)),
             dma((2, chunks)),
-            dma((2, groups, max(cores - 1, 1))),
+            dma((2, groups, 2, others)),
             dma((2, groups, bits, bits)),
             dma((2, groups, bits, bits)),
             dma((max(n - 1, 1),)),
@@ -535,20 +598,14 @@
         compiler_params=pltpu.CompilerParams(
             collective_id=0, has_side_effects=True, vmem_limit_bytes=67043328
         ),
-    )(
-        query_lex.reshape(passes, cores, plan.block, plan.lex),
-        query_dense.reshape(passes, cores, plan.block, plan.dense),
-        passage_lex,
-        passage_dense,
-        pos,
+    )(lex_rows, dense_rows, passage_lex, passage_dense, pos)
+    own_queries = plan.queries // n
+    loss = loss[:, :, 0, :HALF].reshape(2, groups, cores, passes, plan.rows).transpose(3, 2, 0, 1, 4).reshape(-1)
+    loss_rows = lax.dynamic_slice_in_dim(loss, lax.axis_index("red") * own_queries, own_queries)
+    grad_passage_lex, grad_passage_dense = (
+        jnp.dot(left[t], rows.reshape(plan.queries, -1), preferred_element_type=F32)
+        for t, rows in enumerate((lex_ordered, dense_ordered))
     )
-    own_queries = plan.queries // n
-    loss = loss[:, :, 0].reshape(2, groups, cores, passes, plan.rows).transpose(3, 2, 0, 1, 4).reshape(-1)
-    loss_rows = lax.dynamic_slice_in_dim(loss, lax.axis_index("red") * own_queries, own_queries)
-    whole = grads.reshape(2, groups, cores, 2, plan.passages, passes, plan.rows)
-    whole = whole.transpose(3, 4, 5, 2, 0, 1, 6).reshape(2, plan.passages, plan.queries)
-    grad_passage_lex = jnp.dot(whole[0], query_lex, preferred_element_type=F32)
-    grad_passage_dense = jnp.dot(whole[1], query_dense, preferred_element_type=F32)
     return (
         loss_rows,
         gql.reshape(plan.block, plan.lex),

time: 201 us -> 183 us (0.910)
  Pallas kernels: 176 us -> 158 us
  local copies, waits for them, and re-layouts: 12.3 us -> 5.21 us
  matrix products: 12.3 us -> 17.6 us
    pallas_call x1, Pallas kernels: 176 us -> 158 us  [on_device(): pl.pallas_call(functools.partial(fused, plan), out_shape=(jax.ShapeDtypeS...]
    dot_general x2, matrix products: 12.3 us -> 17.6 us  [on_device(): jnp.dot(left[t], rows.reshape(plan.queries, -1), preferred_element_type=F32)]
    pallas_call x1 -> x0, local copies, waits for them, and re-layouts: 3.18 us -> none  [on_device(): pl.pallas_call(functools.partial(fused, plan), out_shape=(jax.ShapeDtypeS...]
    unnamed x14 -> x8, local copies, waits for them, and re-layouts: 5.45 us -> 2.56 us
where the time goes in v2:
time: 183 us
  Pallas kernels  158 us (86%)
  matrix products  17.6 us (10%)
  local copies, waits for them, and re-layouts  5.21 us (3%)
    pallas_call x1, Pallas kernels, on_device(): pl.pallas_call(functools.partial(fused, plan), out_shape=(jax.ShapeDtypeS...  158 us
    dot_general x2, matrix products, on_device(): jnp.dot(left[t], rows.reshape(plan.queries, -1), preferred_element_type=F32)  17.6 us

profile of v2, /device:TPU:1, one launch (start us, length us, event | category | flops | bytes accessed | tf_op | source)
XLA Modules:
  0.0 182.6 jit_solution(16515724494922085365)
XLA Ops:
  0.6 0.8 reshape.39
  1.4 0.1 reshape.40
  1.5 0.7 pad_add_fusion.pos_ref
  2.2 158.4 %shard_map.92 = (f32[2,12,8,128]{3,2,1,0:T(8,128)}, f32[2,3,32,4096]{3,2,1,0:T(8,128)}, f32[2,3,32,1024]{3,2,1,0:T(8,128)}, bf16[2,512,1536]{2,1,0:T(8,128)(2,1)...) custom-call(bf16[4,2,192,4096]{3,2,1,0:T(8,128)(2,1)} %bitcast.18, ...), custom_call_target="tpu_custom_call" | custom-call | tf_op jit(solution)/shard_map/pallas_call | solution.py:552
  160.6 0.9 slice_reduce_fusion
  161.5 0.1 reshape_squeeze.3
  161.6 0.1 reshape.41
  161.7 0.7 dynamic_slice.3
  162.4 0.0 copy-start.2
  162.4 5.6 %fusion = f32[512,1024]{1,0:T(8,128)} fusion(bf16[1536,1024]{1,0:T(8,128)(2,1)} %bitcast.25, bf16[2,512,1536]{2,1,0:T(8,128)(2,1)} %get-tuple-element.14), kind=kOutput, calls=%fused_computation | convolution fusion | flops 1610612736 | bytes 6815744 | tf_op jit(solution)/shard_map/dot_general | solution.py:606
  168.0 0.0 copy-done.2
  168.0 0.0 copy-start
  168.0 12.0 %fusion.2 = f32[512,4096]{1,0:T(8,128)} fusion(bf16[1536,4096]{1,0:T(8,128)(2,1)} %bitcast.24, bf16[2,512,1536]{2,1,0:T(8,128)(2,1)S(1)} %copy-done.2), kind=kOutput, calls=%fused_computation.2 | convolution fusion | flops 6442450944 | bytes 22544384 | tf_op jit(solution)/shard_map/dot_general | solution.py:606
  180.0 0.0 copy-done
  180.0 0.0 copy-start.1
  180.0 1.7 copy.16
  181.7 0.0 copy-done.1
  181.7 0.9 copy.17
  (2 shorter events, 0.0 us)
Async XLA Ops:
  162.4 5.6 %copy-start.2 = (bf16[2,512,1536]{2,1,0:T(8,128)(2,1)S(1)}, bf16[2,512,1536]{2,1,0:T(8,128)(2,1)}, u32[]{:S(2)}) copy-start(bf16[2,512,1536]{2,1,0:T(8,128)(2,1)} %get-tuple-element.14) | copy-start | bytes 9437188
  168.0 12.0 %copy-start = (f32[2,3,32,4096]{3,2,1,0:T(8,128)S(1)}, f32[2,3,32,4096]{3,2,1,0:T(8,128)}, u32[]{:S(2)}) copy-start(f32[2,3,32,4096]{3,2,1,0:T(8,128)} %get-tuple-element.12) | copy-start | bytes 9437188
  180.0 1.7 copy-start.1

commit v3 on v2

--- a/solution.py
+++ b/solution.py
@@ -37,7 +37,9 @@
         self.edges = [(s * tiles // self.bits) * self.tile for s in range(self.bits)] + [self.columns]
         self.lag = 2
         self.keep_slots = -(-self.bits * self.lag // (2 * self.cores))
-        self.parts = 2
+        self.parts = 4
+        self.grad_parts = 2
+        self.own_slots = 1 + self.red // 2
         assert self.passes == 1 << self.bits and self.passes > 1
         assert self.groups * self.rows * 2 == self.block
         assert self.lex % self.tile == 0 and self.dense % self.tile == 0
@@ -47,7 +49,7 @@
 def fused(
     plan,
     ql_hbm, qd_hbm, pl_hbm, pd_hbm, pos_ref,
-    loss_out, gql_out, gqd_out, left_out, qlp_out, qdp_out,
+    loss_out, gql_out, gqd_out, left_lex_out, left_dense_out, qlp_out, qdp_out,
     qlv, qdv, plv, pdv, rs, own, grad, left, gx, st, lossb, tsend, trecv, keep,
     q_sem, p_sem, o_sem, w_sem, ps_sem, pr_sem, rss_sem, rsr_sem, sts_sem, str_sem, gs_sem, gr_sem,
     xs_sem, xr_sem, ts_sem, tr_sem, ls_sem, lr_sem,
@@ -69,7 +71,7 @@
         start = d * plan.half + group * plan.rows
         return pltpu.make_async_copy(
             source.at[:, core, pl.ds(pl.multiple_of(start, plan.rows), plan.rows), :],
-            target.at[d, c],
+            target.at[c, d],
             q_sem.at[d, c, t],
         )
 
@@ -110,22 +112,25 @@
             device_id_type=MESH,
         )
 
-    def g_copy(d, c):
+    def g_copy(d, u, part):
+        size = plan.passages // plan.grad_parts
+        where = (d, u, pl.ds(part * size, size))
         return pltpu.make_async_remote_copy(
-            src_ref=grad.at[d, c],
-            dst_ref=grad.at[d, c],
-            send_sem=gs_sem.at[d, c],
-            recv_sem=gr_sem.at[d, c],
+            src_ref=grad.at[where],
+            dst_ref=grad.at[where],
+            send_sem=gs_sem.at[d, u, part],
+            recv_sem=gr_sem.at[d, u, part],
             device_id={"red": back[d]},
             device_id_type=MESH,
         )
 
-    def left_store(d, c):
+    def left_store(d, c, t):
         where = pl.ds(pl.multiple_of((d * pairs + c) * LANES, LANES), LANES)
-        return pltpu.make_async_copy(left.at[:, :, where], left_out.at[:, :, where], o_sem.at[d, c])
+        out = (left_lex_out, left_dense_out)[t]
+        return pltpu.make_async_copy(left.at[t, :, where], out.at[:, where], o_sem.at[d, c, t])
 
     def q_store(d, c, t):
-        return pltpu.make_async_copy((qlv, qdv)[t].at[d, c], (qlp_out, qdp_out)[t].at[d, c], w_sem.at[d, c, t])
+        return pltpu.make_async_copy((qlv, qdv)[t].at[c, d], (qlp_out, qdp_out)[t].at[d, c], w_sem.at[d, c, t])
 
     def x_copy(d, u, slot, target):
         group = u // (2 * cores)
@@ -204,23 +209,26 @@
     def swap(values):
         return pltpu.roll(values, HALF, 1)
 
-    def own_scores(d, c):
+    def own_scores(c):
         totals = []
         for t in range(2):
-            local_q(d, c, t).wait()
-            q_store(d, c, t).start()
-            rows = (qlv, qdv)[t][d, c].reshape(LANES, (plan.lex, plan.dense)[t])
+            for d in range(2):
+                local_q(d, c, t).wait()
+                q_store(d, c, t).start()
+            rows = (qlv, qdv)[t][c].reshape(2 * LANES, (plan.lex, plan.dense)[t])
             totals.append(lax.dot_general(
                 (plv, pdv)[t][my_core], rows, (((1,), (1,)), ((), ())), preferred_element_type=F32
             ))
-        lexical, dense = totals
-        own[d, 0] = jnp.where(low, lexical, swap(dense))
-        own[d, 1] = jnp.where(low, swap(lexical), dense)
+        slot = lax.rem(c, plan.own_slots)
+        for d in range(2):
+            lexical, dense = (total[:, d * LANES:(d + 1) * LANES] for total in totals)
+            own[d, slot, 0] = jnp.where(low, lexical, swap(dense))
+            own[d, slot, 1] = jnp.where(low, swap(lexical), dense)
 
     def add_scores(d, u, part):
         size = plan.passages // plan.parts
         where = pl.ds(part * size, size)
-        mine = own.at[d, lax.rem(u, 2), where]
+        mine = own.at[d, lax.rem(u // 2, plan.own_slots), lax.rem(u, 2), where]
         rs_now = rs.at[d, u, where]
 
         @pl.when(hops[d] > 0)
@@ -384,7 +392,8 @@
         where = pl.ds(pl.multiple_of((d * pairs + c) * LANES, LANES), LANES)
         left[0, :, where] = jnp.where(low, halves[0], swap(halves[1])).astype(BF16)
         left[1, :, where] = jnp.where(low, swap(halves[0]), halves[1]).astype(BF16)
-        left_store(d, c).start()
+        for t in range(2):
+            left_store(d, c, t).start()
 
     def inside(u):
         return jnp.logical_and(u >= 0, u < chunks)
@@ -422,14 +431,15 @@
 
                 terms(d, c)
 
+        soonest = tau - jnp.minimum(hops[0], hops[1])
+
+        @pl.when(jnp.logical_and(inside(soonest), lax.rem(soonest, 2) == 0))
+        def _():
+            own_scores(soonest // 2)
+
         for part in range(plan.parts):
             for d in range(2):
                 u = tau - hops[d]
-                if part == 0:
-                    @pl.when(jnp.logical_and(inside(u), lax.rem(u, 2) == 0))
-                    def _(d=d, u=u):
-                        own_scores(d, u // 2)
-
                 @pl.when(inside(u))
                 def _(d=d, u=u, part=part):
                     add_scores(d, u, part)
@@ -459,13 +469,14 @@
 
             @pl.when(inside(u))
             def _(d=d, u=u, away=away):
-                @pl.when(away > 0)
-                def _():
-                    g_copy(d, u).wait_recv()
-
-                @pl.when(away < n - 1)
-                def _():
-                    g_copy(d, u).start()
+                for part in range(plan.grad_parts):
+                    @pl.when(away > 0)
+                    def _(part=part):
+                        g_copy(d, u, part).wait_recv()
+
+                    @pl.when(away < n - 1)
+                    def _(part=part):
+                        g_copy(d, u, part).start()
 
                 core = lax.rem(u // 2, cores)
 
@@ -505,7 +516,8 @@
 
             @pl.when(hops[d] > 0)
             def _():
-                g_copy(d, c).wait_send()
+                for part in range(plan.grad_parts):
+                    g_copy(d, c, part).wait_send()
 
             @pl.when(hops[d] == n - 1)
             def _():
@@ -532,8 +544,8 @@
             send_p(k, t).wait_send()
     for d in range(2):
         for c in range(pairs):
-            left_store(d, c).wait()
             for t in range(2):
+                left_store(d, c, t).wait()
                 q_store(d, c, t).wait()
     loss_out[...] = lossb[...]
 
@@ -549,25 +561,26 @@
     others = max(cores - 1, 1)
     lex_rows = query_lex.reshape(passes, cores, plan.block, plan.lex)
     dense_rows = query_dense.reshape(passes, cores, plan.block, plan.dense)
-    loss, gql, gqd, left, lex_ordered, dense_ordered = pl.pallas_call(
+    loss, gql, gqd, left_lex, left_dense, lex_ordered, dense_ordered = pl.pallas_call(
         functools.partial(fused, plan),
         out_shape=(
             jax.ShapeDtypeStruct((2, chunks, 8, LANES), F32),
             jax.ShapeDtypeStruct((2, groups, plan.rows, plan.lex), F32),
             jax.ShapeDtypeStruct((2, groups, plan.rows, plan.dense), F32),
-            jax.ShapeDtypeStruct((2, plan.passages, plan.queries), BF16),
+            jax.ShapeDtypeStruct((plan.passages, plan.queries), BF16),
+            jax.ShapeDtypeStruct((plan.passages, plan.queries), BF16),
             jax.ShapeDtypeStruct((2, plan.pairs, passes, plan.rows, plan.lex), BF16),
             jax.ShapeDtypeStruct((2, plan.pairs, passes, plan.rows, plan.dense), BF16),
         ),
         in_specs=[any_space, any_space, any_space, any_space, vmem],
-        out_specs=(vmem, vmem, vmem, any_space, any_space, any_space),
+        out_specs=(vmem, vmem, vmem, any_space, any_space, any_space, any_space),
         scratch_shapes=[
-            pltpu.VMEM((2, plan.pairs, passes, plan.rows, plan.lex), BF16),
-            pltpu.VMEM((2, plan.pairs, passes, plan.rows, plan.dense), BF16),
+            pltpu.VMEM((plan.pairs, 2, passes, plan.rows, plan.lex), BF16),
+            pltpu.VMEM((plan.pairs, 2, passes, plan.rows, plan.dense), BF16),
             pltpu.VMEM((cores, plan.passages, plan.lex), BF16),
             pltpu.VMEM((cores, plan.passages, plan.dense), BF16),
             pltpu.VMEM((2, chunks, plan.passages, LANES), F32),
-            pltpu.VMEM((2, 2, plan.passages, LANES), F32),
+            pltpu.VMEM((2, plan.own_slots, 2, plan.passages, LANES), F32),
             pltpu.VMEM((2, chunks, plan.passages, LANES), BF16),
             pltpu.VMEM((2, plan.passages, plan.queries), BF16),
             pltpu.VMEM((2, groups, 2, others, plan.passages, LANES), BF16),
@@ -578,7 +591,7 @@
             pltpu.VMEM((2, plan.keep_slots, passes // 2, plan.rows, plan.columns), F32),
             dma((2, plan.pairs, 2)),
             dma((2,)),
-            dma((2, plan.pairs)),
+            dma((2, plan.pairs, 2)),
             dma((2, plan.pairs, 2)),
             dma((others, 2)),
             dma((others, 2)),
@@ -586,8 +599,8 @@
             dma((2, chunks, plan.parts)),
             dma((chunks, plan.plane - 1)),
             dma((chunks, plan.plane - 1)),
-            dma((2, chunks)),
-            dma((2, chunks)),
+            dma((2, chunks, plan.grad_parts)),
+            dma((2, chunks, plan.grad_parts)),
             dma((2, chunks)),
             dma((2, groups, 2, others)),
             dma((2, groups, bits, bits)),
@@ -603,8 +616,8 @@
     loss = loss[:, :, 0, :HALF].reshape(2, groups, cores, passes, plan.rows).transpose(3, 2, 0, 1, 4).reshape(-1)
     loss_rows = lax.dynamic_slice_in_dim(loss, lax.axis_index("red") * own_queries, own_queries)
     grad_passage_lex, grad_passage_dense = (
-        jnp.dot(left[t], rows.reshape(plan.queries, -1), preferred_element_type=F32)
-        for t, rows in enumerate((lex_ordered, dense_ordered))
+        jnp.dot(left, rows.reshape(plan.queries, -1), preferred_element_type=F32)
+        for left, rows in ((left_lex, lex_ordered), (left_dense, dense_ordered))
     )
     return (
         loss_rows,

time: 183 us -> 182 us (level)
  no operation moved by 1% of the time
where the time goes in v3:
time: 182 us; the launch traced here: 181 us
  Pallas kernels  158 us (87%)
  matrix products  17.4 us (10%)
  local copies, waits for them, and re-layouts  5.21 us (3%)
    pallas_call x1, Pallas kernels, on_device(): pl.pallas_call(functools.partial(fused, plan), out_shape=(jax.ShapeDtypeS...  158 us
    dot_general x2, matrix products, on_device(): jnp.dot(left, rows.reshape(plan.queries, -1), preferred_element_type=F32)  17.4 us

profile of v3, /device:TPU:1, one launch (start us, length us, event | category | flops | bytes accessed | tf_op | source)
XLA Modules:
  0.0 181.5 jit_solution(7185854091789444825)
XLA Ops:
  0.6 0.8 reshape.39
  1.4 0.1 reshape.40
  1.5 0.7 pad_add_fusion.pos_ref
  2.2 157.5 %shard_map.92 = (f32[2,12,8,128]{3,2,1,0:T(8,128)}, f32[2,3,32,4096]{3,2,1,0:T(8,128)}, f32[2,3,32,1024]{3,2,1,0:T(8,128)}, bf16[512,1536]{1,0:T(8,128)(2,1)}, b...) custom-call(bf16[4,2,192,4096]{3,2,1,0:T(8,128)(2,1)} %bitcast.14, ...), custom_call_target="tpu_custom_call" | custom-call | tf_op jit(solution)/shard_map/pallas_call | solution.py:564
  159.8 0.9 slice_reduce_fusion
  160.7 0.1 reshape_squeeze.3
  160.8 0.1 reshape.41
  160.9 0.7 dynamic_slice.3
  161.5 0.0 copy-start.2
  161.5 5.6 %fusion.1 = f32[512,1024]{1,0:T(8,128)} fusion(bf16[512,1536]{1,0:T(8,128)(2,1)} %get-tuple-element.17, bf16[1536,1024]{1,0:T(8,128)(2,1)} %bitcast.21), kind=kOutput, calls=%fused_computation.4 | convolution fusion | flops 1610612736 | bytes 6815744 | tf_op jit(solution)/shard_map/dot_general | solution.py:619
  167.1 0.0 copy-done.2
  167.1 0.0 copy-start
  167.1 11.8 %fusion = f32[512,4096]{1,0:T(8,128)} fusion(bf16[512,1536]{1,0:T(8,128)(2,1)S(1)} %copy-done.2, bf16[1536,4096]{1,0:T(8,128)(2,1)} %bitcast.20), kind=kOutput, calls=%fused_computation.3 | convolution fusion | flops 6442450944 | bytes 22544384 | tf_op jit(solution)/shard_map/dot_general | solution.py:619
  178.9 0.0 copy-done
  178.9 0.0 copy-start.1
  178.9 1.7 copy.16
  180.6 0.0 copy-done.1
  180.6 0.9 copy.17
  (2 shorter events, 0.0 us)
Async XLA Ops:
  161.5 5.6 %copy-start.2 = (bf16[512,1536]{1,0:T(8,128)(2,1)S(1)}, bf16[512,1536]{1,0:T(8,128)(2,1)}, u32[]{:S(2)}) copy-start(bf16[512,1536]{1,0:T(8,128)(2,1)} %get-tuple-element.15) | copy-start | bytes 4718596
  167.1 11.8 %copy-start = (f32[2,3,32,4096]{3,2,1,0:T(8,128)S(1)}, f32[2,3,32,4096]{3,2,1,0:T(8,128)}, u32[]{:S(2)}) copy-start(f32[2,3,32,4096]{3,2,1,0:T(8,128)} %get-tuple-element.13) | copy-start | bytes 9437188
  178.9 1.7 copy-start.1
